TPU v7x, 32 devices: a 4x2x2 block of a 4x4x8 slice. The times are simulated.
32 devices in a mesh: dp: 4 (over y, z), ep: 8 (over x, core).
Axes of the slice: x: 4, y: 2, z: 2, core: 2. Of those that a mesh axis runs over, the one named last changes fastest.
The devices are a block of a 4x4x8 slice.
Arguments:
- x_tok: bfloat16 [32, 512, 2048], P(('dp', 'ep')), parts along dimension 0
- w_query: bfloat16 [2048, 16, 128], P('ep')
- w_key: bfloat16 [2048, 16, 128], P('ep')
- w_value: bfloat16 [2048, 16, 128], P('ep')
- w_out: bfloat16 [2048, 2048], P('ep')
- w_router: float32 [2048, 64], replicated
- w_gate: bfloat16 [64, 2048, 1024], P('ep')
- w_up: bfloat16 [64, 2048, 1024], P('ep')
- w_down: bfloat16 [64, 1024, 2048], P('ep')
- ws_gate: bfloat16 [2048, 1024], P('ep')
- ws_up: bfloat16 [2048, 1024], P('ep')
- ws_down: bfloat16 [1024, 2048], P('ep')
- expert_ids: int32 [32, 512, 8], P(('dp', 'ep')), parts along dimension 0
Outputs:
- output: bfloat16 [32, 512, 2048], P(('dp', 'ep')), parts along dimension 0
There are 4 independent parts. A program takes and returns all parts, laid end to end along the dimension named above; an argument that names none is the same for every part.
All inputs are finite; a program needn't handle non-finite values.
Results may differ from a plain program's by a relative error of at most 0.0133186.
Values are sent between devices in bfloat16 or wider.
A program may use at most 768 MiB of HBM per device.

v0:
```python
import functools
import jax
import jax.numpy as jnp
from jax import lax
from jax.sharding import PartitionSpec as P

EPSILON = 1e-6
CAP_FACTOR = 2


def rms_norm(values):
    as_f32 = values.astype(jnp.float32)
    return as_f32 * lax.rsqrt(jnp.mean(as_f32 * as_f32, axis=-1, keepdims=True) + EPSILON)


def swiglu_rows(row_block, gate_w, up_w, down_w):
    gate_act = jnp.einsum('...d,df->...f', row_block, gate_w, preferred_element_type=jnp.float32)
    up_act = jnp.einsum('...d,df->...f', row_block, up_w, preferred_element_type=jnp.float32)
    middle = (jax.nn.silu(gate_act) * up_act).astype(jnp.bfloat16)
    return jnp.einsum('...f,fd->...d', middle, down_w, preferred_element_type=jnp.float32).astype(jnp.bfloat16)


def slot_plan(flat_ids, n_experts, capacity, top_k):
    n_assign = flat_ids.shape[0]
    sort_order = jnp.argsort(flat_ids, stable=True)
    expert_counts = jnp.bincount(flat_ids, length=n_experts)
    expert_starts = jnp.cumsum(expert_counts) - expert_counts
    slot_rows = jnp.minimum(expert_starts[:, None] + jnp.arange(capacity)[None, :], n_assign - 1)
    slot_token = jnp.take(sort_order, slot_rows.reshape(-1)) // top_k
    rank_of = jnp.argsort(sort_order)
    slot_of_assign = flat_ids * capacity + rank_of - jnp.take(expert_starts, flat_ids)
    return slot_token, slot_of_assign


def attention_block(x_loc, query_w, key_w, value_w, out_w):
    n_seq, seq_len, d_model = x_loc.shape
    head_dim = query_w.shape[2]
    normed = rms_norm(x_loc).astype(jnp.bfloat16)
    queries = jnp.einsum('bsd,dhe->bshe', normed, query_w, preferred_element_type=jnp.float32).astype(jnp.bfloat16)
    keys_all = jnp.einsum('bsd,dhe->bshe', normed, key_w, preferred_element_type=jnp.float32).astype(jnp.bfloat16)
    vals_all = jnp.einsum('bsd,dhe->bshe', normed, value_w, preferred_element_type=jnp.float32).astype(jnp.bfloat16)
    scores = jnp.einsum('bqhe,bkhe->bhqk', queries, keys_all, preferred_element_type=jnp.float32) * (head_dim ** -0.5)
    causal = jnp.arange(seq_len)[:, None] >= jnp.arange(seq_len)[None, :]
    attn_probs = jax.nn.softmax(jnp.where(causal, scores, -1e30), axis=-1).astype(jnp.bfloat16)
    attended = jnp.einsum('bhqk,bkhe->bqhe', attn_probs, vals_all, preferred_element_type=jnp.float32).astype(jnp.bfloat16)
    attn_out = jnp.einsum('crx,xe->cre', attended.reshape(n_seq, seq_len, -1), out_w, preferred_element_type=jnp.float32).astype(jnp.bfloat16)
    return (x_loc.astype(jnp.float32) + attn_out.astype(jnp.float32)).astype(jnp.bfloat16)


def local_layer(x_loc, q_shard, k_shard, v_shard, o_shard, w_router, gate_loc, up_loc, down_loc, sgate_shard, sup_shard, sdown_shard, ids_loc, group):
    query_w = lax.all_gather(q_shard, 'ep', axis=0, tiled=True)
    key_w = lax.all_gather(k_shard, 'ep', axis=0, tiled=True)
    value_w = lax.all_gather(v_shard, 'ep', axis=0, tiled=True)
    out_w = lax.all_gather(o_shard, 'ep', axis=0, tiled=True)
    residual = attention_block(x_loc, query_w, key_w, value_w, out_w)
    n_seq, seq_len, d_model = x_loc.shape
    n_tok = n_seq * seq_len
    top_k = ids_loc.shape[-1]
    local_experts = gate_loc.shape[0]
    n_experts = local_experts * group
    capacity = CAP_FACTOR * n_tok * top_k // n_experts
    hidden = rms_norm(residual).reshape(n_tok, d_model)
    tok_ids = ids_loc.reshape(n_tok, top_k)
    logits = jnp.dot(hidden, w_router, precision=lax.Precision.HIGHEST, preferred_element_type=jnp.float32)
    gate_probs = jax.nn.softmax(jnp.take_along_axis(logits, tok_ids, axis=1), axis=-1)
    moe_in = hidden.astype(jnp.bfloat16)
    slot_token, slot_of_assign = slot_plan(tok_ids.reshape(-1), n_experts, capacity, top_k)
    send_buf = jnp.take(moe_in, slot_token, axis=0).reshape(group, local_experts, capacity, d_model)
    received = lax.all_to_all(send_buf, 'ep', 0, 2, tiled=True).reshape(local_experts, group * capacity, d_model)
    gate_act = jnp.einsum('ecd,edf->ecf', received, gate_loc, preferred_element_type=jnp.float32)
    up_act = jnp.einsum('ecd,edf->ecf', received, up_loc, preferred_element_type=jnp.float32)
    middle = (jax.nn.silu(gate_act) * up_act).astype(jnp.bfloat16)
    expert_out = jnp.einsum('ecf,efd->ecd', middle, down_loc, preferred_element_type=jnp.float32).astype(jnp.bfloat16)
    returned = lax.all_to_all(expert_out.reshape(1, local_experts, group * capacity, d_model), 'ep', 2, 0, tiled=True)
    picked_rows = jnp.take(returned.reshape(n_experts * capacity, d_model), slot_of_assign, axis=0).reshape(n_tok, top_k, d_model)
    routed = jnp.sum(picked_rows.astype(jnp.float32) * gate_probs[:, :, None], axis=1)
    shared_gate = lax.all_gather(sgate_shard, 'ep', axis=0, tiled=True)
    shared_up = lax.all_gather(sup_shard, 'ep', axis=0, tiled=True)
    shared_down = lax.all_gather(sdown_shard, 'ep', axis=0, tiled=True)
    shared = swiglu_rows(moe_in, shared_gate, shared_up, shared_down)
    y_out = (residual.reshape(n_tok, d_model).astype(jnp.float32) + routed + shared.astype(jnp.float32)).astype(jnp.bfloat16)
    return y_out.reshape(n_seq, seq_len, d_model)


def solution(mesh):
    tok_spec = P(('dp', 'ep'), None, None)
    row_spec = P('ep', None)
    cube_spec = P('ep', None, None)
    in_specs = (tok_spec, cube_spec, cube_spec, cube_spec, row_spec, P(None, None), cube_spec, cube_spec, cube_spec, row_spec, row_spec, row_spec, tok_spec)
    return jax.shard_map(functools.partial(local_layer, group=mesh.shape['ep']), mesh=mesh, in_specs=in_specs, out_specs=tok_spec, check_vma=False)
```

profile of v0, /device:TPU:81, one launch (start us, length us, event | category | flops | bytes accessed | tf_op | source)
XLA Modules:
  0.0 1433.3 jit_solution(12912534439987062912)
XLA Ops:
  10.1 28.9 %scatter_custom_fusion = s32[64]{0:T(128)S(1)} fusion(s32[4096]{0:T(1024)S(1)} %bitcast.168, s32[4096]{0:T(1024)S(1)} %broadcast.488, s32[]{:T(128)} %constant.103.clone.1), kind=kCustom, calls=%fused_computation.160 | custom fusion | flops 4096 | bytes 260 | tf_op jit(solution)/shard_map/scatter-add | solution.py:26
  45.4 45.5 %gather_fusion = s32[8192]{0:T(1024)S(1)} fusion(s32[4096]{0:T(1024)S(1)} %get-tuple-element.7, s32[8192]{0:T(1024)S(1)} %broadcast_clamp_fusion.1), kind=kCustom, calls=%fused_computation | custom fusion | bytes 98304 | tf_op jit(solution)/shard_map/jit(_take)/gather | solution.py:29
  91.9 9.3 fusion.4
  108.3 12.7 fusion.27
  121.0 17.2 %fusion.70 = (f32[16,512]{1,0:T(8,128)S(1)}, f32[16,512,512]{1,2,0:T(8,128)}) fusion(f32[16,512,512]{1,2,0:T(8,128)} %fusion.27, pred[512,512]{0,1:T(8,128)(4,1)S(1)} %iota_compare_fusion), kind=kOutput, calls=%fused_computation.170 | output fusion | flops 25166336 | bytes 33849344 | tf_op jit(solution)/shard_map/sub | solution.py:44
  138.2 18.4 %all-gather.8.cloned.1.call-done = bf16[2048,16,128]{2,1,0:T(8,128)(2,1)} async-done(((bf16[256,16,128]{2,1,0:T(8,128)(2,1)}), bf16[2048,16,128]{2,1,0:T(8,128)(2,1)}) %all-gather.8.cloned.1.call-update) | async-done | bytes 8388624 | tf_op jit(solution)/shard_map/all_gather | solution.py:53
  156.6 12.6 fusion.39
  169.2 35.5 %all-gather.14.cloned.1.call-done = bf16[2048,2048]{1,0:T(8,128)(2,1)} async-done(((bf16[256,2048]{1,0:T(8,128)(2,1)}), bf16[2048,2048]{1,0:T(8,128)(2,1)}) %all-gather.14.cloned.1.call-update) | async-done | bytes 8388624 | tf_op jit(solution)/shard_map/all_gather | solution.py:54
  204.7 9.1 fusion.18
  215.6 40.5 %gather_fusion.1 = bf16[8192,2048]{1,0:T(8,128)(2,1)} fusion(bf16[512,2048]{1,0:T(8,128)(2,1)S(1)} %fusion.22, s32[8192]{0:T(1024)S(1)} %broadcast_clamp_fusion), kind=kCustom, calls=%fused_computation.1 | custom fusion | bytes 67141632 | tf_op jit(solution)/shard_map/jit(_take)/gather | solution.py:68
  256.1 22.9 %broadcast_select_fusion = bf16[8,8,128,2048]{3,2,1,0:T(8,128)(2,1)} fusion(bf16[8,8,128,2048]{3,2,1,0:T(8,128)(2,1)} %bitcast.158, pred[8,8,128]{2,1,0:T(8,128)(4,1)S(1)} %compare_and_fusion), kind=kLoop, calls=%fused_computation.9 | loop fusion | flops 16777216 | bytes 67117056 | tf_op jit(solution)/shard_map/jit(_take)/select_n | solution.py:68
  278.9 374.9 %all_to_all.30 = bf16[8,8,128,2048]{3,2,1,0:T(8,128)(2,1)} all-to-all(bf16[8,8,128,2048]{3,2,1,0:T(8,128)(2,1)} %broadcast_select_fusion), channel_id=1, replica_groups=mesh['dp'=4,'ep'=8] {'ep'}, dimensions={0} | all-to-all | bytes 67108864 | tf_op jit(solution)/shard_map/all_to_all | solution.py:69
  653.9 22.9 %copy.37 = bf16[1,8,8,128,2048]{4,3,2,1,0:T(8,128)(2,1)} copy(bf16[1,8,8,128,2048]{4,3,1,2,0:T(8,128)(2,1)} %bitcast.159) | data formatting | bytes 67108864 | tf_op jit(solution)/shard_map/all_to_all | solution.py:69
  676.8 44.3 %fusion.75 = f32[8,1024,1024]{2,1,0:T(8,128)} fusion(bf16[8,1024,2048]{2,1,0:T(8,128)(2,1)} %bitcast.160, bf16[8,2048,1024]{2,1,0:T(8,128)(2,1)} %param.19), kind=kOutput, calls=%fused_computation.172 | convolution fusion | flops 34359738368 | bytes 100663296 | tf_op jit(solution)/shard_map/ecd,edf->ecf/dot_general | solution.py:70
  721.0 53.8 %multiply_convert_fusion = bf16[8,1024,1024]{2,1,0:T(8,128)(2,1)} fusion(f32[8,1024,1024]{2,1,0:T(8,128)} %fusion.75, bf16[8,1024,2048]{2,1,0:T(8,128)(2,1)} %bitcast.161, bf16[8,2048,1024]{2,1,0:T(8,128)(2,1)} %param.20), kind=kOutput, calls=%fused_computation.8 | convolution fusion | flops 34410070016 | bytes 117440512 | tf_op jit(solution)/shard_map/ecd,edf->ecf/dot_general | solution.py:71
  774.8 43.4 %convert_bitcast_fusion = bf16[1,8,1024,2048]{3,2,1,0:T(8,128)(2,1)} fusion(bf16[8,1024,1024]{2,1,0:T(8,128)(2,1)} %multiply_convert_fusion, bf16[8,1024,2048]{2,1,0:T(8,128)(2,1)} %param.21), kind=kOutput, calls=%fused_computation.7 | convolution fusion | flops 34376515584 | bytes 83886080 | tf_op jit(solution)/shard_map/ecf,efd->ecd/dot_general | solution.py:73
  818.2 30.0 %copy.38 = bf16[1,8,1024,2048]{3,1,0,2:T(8,128)(2,1)} copy(bf16[1,8,1024,2048]{3,2,1,0:T(8,128)(2,1)} %convert_bitcast_fusion) | data formatting | bytes 67108864 | tf_op jit(solution)/shard_map/reshape | solution.py:74
  874.4 35.7 %compare_and_fusion.1 = (pred[4096]{0:T(1024)(128)(4,1)S(1)}, s32[4096]{0:T(1024)S(1)}) fusion(pred[4096]{0:T(1024)(128)(4,1)S(1)} %get-tuple-element.65, pred[4096]{0:T(1024)(128)(4,1)S(1)} %get-tuple-element.64, pred[4096]{0:T(1024)(128)(4,1)S(1)} %get-tuple-element.63, pred[4096]{0:T(1024)(128)(4,1)S(1)} %get-tuple-element.62, ...), kind=kLoop, calls=%fused_computation.155 | loop fusion | flops 299008 | bytes 303332 | tf_op jit(solution)/shard_map/jit(_take)/and | solution.py:75
  915.1 33.3 %gather_fusion.3 = f32[4096]{0:T(1024)S(1)} fusion(f32[512,64]{0,1:T(8,128)S(1)} %fusion.20, s32[4096]{0:T(1024)S(1)} %reshape.514), kind=kCustom, calls=%fused_computation.3 | custom fusion | bytes 65536 | tf_op jit(solution)/shard_map/jit(take_along_axis)/gather | solution.py:65
  955.8 314.4 %all-to-all-done.1 = bf16[1,8,1024,2048]{3,1,0,2:T(8,128)(2,1)} async-done(((bf16[1,8,1024,2048]{3,1,0,2:T(8,128)(2,1)}), bf16[1,8,1024,2048]{3,1,0,2:T(8,128)(2,1)}, u32[]{:S(2)}, u32[]{:S(2)}) %all-to-all-start.1) | async-done | bytes 33554464 | tf_op jit(solution)/shard_map/all_to_all | solution.py:74
  1270.2 30.0 %copy.39 = bf16[1,8,8,128,2048]{4,3,1,2,0:T(8,128)(2,1)} copy(bf16[1,8,8,128,2048]{4,1,3,2,0:T(8,128)(2,1)} %bitcast.85) | data formatting | bytes 67108864 | tf_op jit(solution)/shard_map/all_to_all | solution.py:74
  1300.3 95.9 %gather_fusion.2 = bf16[4096,2048]{1,0:T(8,128)(2,1)} fusion(bf16[8192,2048]{1,0:T(8,128)(2,1)} %bitcast.157, s32[4096]{0:T(1024)S(1)} %broadcast_clamp_fusion.2), kind=kCustom, calls=%fused_computation.2 | custom fusion | bytes 33570816 | tf_op jit(solution)/shard_map/jit(_take)/gather | solution.py:75
  1396.2 18.9 %multiply_reduce_fusion = f32[512,2048]{1,0:T(8,128)} fusion(bf16[4096,2048]{1,0:T(8,128)(2,1)} %gather_fusion.2, f32[512,8]{1,0:T(8,128)S(1)} %copy-done.10, pred[512,8]{1,0:T(8,128)(4,1)S(1)} %broadcast_in_dim.73), kind=kLoop, calls=%fused_computation.6 | loop fusion | flops 32505856 | bytes 20992000 | tf_op jit(solution)/shard_map/reduce_sum | solution.py:76
  1415.1 11.2 fusion.24
  (100 shorter events, 57.8 us)
Async XLA Ops:
  6.5 904.1 %copy-start = (f32[2048,64]{0,1:T(8,128)S(1)}, f32[2048,64]{0,1:T(8,128)}, u32[]{:S(2)}) copy-start(f32[2048,64]{0,1:T(8,128)} %param.18) | copy-start | bytes 1572868
  6.6 85.4 %all-gather.10.cloned.1.call-start = ((), (), s32[]{:S(2)}) async-start(), calls=%async_computation.3 | async-start | bytes 9437184 | tf_op jit(solution)/shard_map/all_gather | solution.py:51
  7.3 101.0 %all-gather.12.cloned.1.call-start = ((), (), s32[]{:S(2)}) async-start(), calls=%async_computation.4 | async-start | bytes 9437184 | tf_op jit(solution)/shard_map/all_gather | solution.py:52
  8.1 148.4 %all-gather.8.cloned.1.call-start = ((), (), s32[]{:S(2)}) async-start(), calls=%async_computation.2 | async-start | bytes 9437184 | tf_op jit(solution)/shard_map/all_gather | solution.py:53
  8.9 195.8 %all-gather.14.cloned.1.call-start = ((), (), s32[]{:S(2)}) async-start(), calls=%async_computation.5 | async-start | bytes 9437184 | tf_op jit(solution)/shard_map/all_gather | solution.py:54
  9.7 29.7 %copy-start.3 = (s32[1,512,8]{2,1,0:T(8,128)}, s32[1,512,8]{2,1,0:T(8,128)S(1)}, u32[]{:S(2)}) copy-start(s32[1,512,8]{2,1,0:T(8,128)S(1)} %copy.34) | copy-start | bytes 49156
  9.9 29.4 %copy-start.11 = (s32[4096,1]{0,1:T(1,128)}, s32[4096,1]{0,1:T(1,128)S(1)}, u32[]{:S(2)}) copy-start(s32[4096,1]{0,1:T(1,128)S(1)} %reshape_reshape.6) | copy-start | bytes 49156
  10.0 35.3 %copy-start.13 = (s32[4096]{0:T(1024)}, s32[4096]{0:T(1024)S(1)}, u32[]{:S(2)}) copy-start(s32[4096]{0:T(1024)S(1)} %reshape_reshape.5) | copy-start | bytes 49156
  39.3 51.6 %copy-start.7 = (s32[64]{0:T(128)}, s32[64]{0:T(128)S(1)}, u32[]{:S(2)}) copy-start(s32[64]{0:T(128)S(1)} %sub.37) | copy-start | bytes 772
  45.2 45.7 %copy-start.1 = (s32[4096]{0:T(1024)}, s32[4096]{0:T(1024)S(1)}, u32[]{:S(2)}) copy-start(s32[4096]{0:T(1024)S(1)} %get-tuple-element.7) | copy-start | bytes 49156
  45.4 45.7 %copy-start.9 = (bf16[1,512,2048]{2,1,0:T(8,128)(2,1)S(1)}, bf16[1,512,2048]{2,1,0:T(8,128)(2,1)}, u32[]{:S(2)}) copy-start(bf16[1,512,2048]{2,1,0:T(8,128)(2,1)} %param.13) | copy-start | bytes 6291460
  213.8 42.2 %copy-start.17 = (f32[512]{0:T(512)}, f32[512]{0:T(512)S(1)}, u32[]{:S(2)}) copy-start(f32[512]{0:T(512)S(1)} %add_rsqrt_fusion) | copy-start | bytes 6148
  848.2 16.1 %copy-start.8 = (s32[64]{0:T(128)S(1)}, s32[64]{0:T(128)}, u32[]{:S(2)}) copy-start(s32[64]{0:T(128)} %copy-done.7) | copy-start | bytes 772
  848.2 18.9 %copy-start.12 = (s32[4096,1]{0,1:T(1,128)S(1)}, s32[4096,1]{0,1:T(1,128)}, u32[]{:S(2)}) copy-start(s32[4096,1]{0,1:T(1,128)} %copy-done.11) | copy-start | bytes 49156
  848.2 26.2 %copy-start.14 = (s32[4096]{0:T(1024)S(1)}, s32[4096]{0:T(1024)}, u32[]{:S(2)}) copy-start(s32[4096]{0:T(1024)} %copy-done.13) | copy-start | bytes 49156
  848.3 62.1 %copy-start.16 = (s32[1,512,8]{1,2,0:T(8,128)S(1)}, s32[1,512,8]{1,2,0:T(8,128)}, u32[]{:S(2)}) copy-start(s32[1,512,8]{1,2,0:T(8,128)} %param.25) | copy-start | bytes 49156
  848.3 62.4 %copy-start.6 = (bf16[1,512,2048]{2,1,0:T(8,128)(2,1)S(1)}, bf16[1,512,2048]{2,1,0:T(8,128)(2,1)}, u32[]{:S(2)}) copy-start(bf16[1,512,2048]{2,1,0:T(8,128)(2,1)} %copy-done.5) | copy-start | bytes 6291460
  848.3 62.4 %copy-start.18 = (f32[512]{0:T(512)S(1)}, f32[512]{0:T(512)}, u32[]{:S(2)}) copy-start(f32[512]{0:T(512)} %copy-done.17) | copy-start | bytes 6148
  848.3 422.0 %all-to-all-start.1 = ((bf16[1,8,1024,2048]{3,1,0,2:T(8,128)(2,1)}), bf16[1,8,1024,2048]{3,1,0,2:T(8,128)(2,1)}, u32[]{:S(2)}, u32[]{:S(2)}) async-start(bf16[1,8,1024,2048]{3,1,0,2:T(8,128)(2,1)} %copy.38), calls=%async_computation.1 | async-start | bytes 67108864 | tf_op jit(solution)/shard_map/all_to_all | solution.py:74
  856.4 93.5 %all-gather.16.cloned.1.call-start = ((), (), s32[]{:S(2)}) async-start(), calls=%async_computation.6 | async-start | bytes 4718592 | tf_op jit(solution)/shard_map/all_gather | solution.py:77
  857.0 558.0 %all-gather.18.cloned.1.call-start = ((), (), s32[]{:S(2)}) async-start(), calls=%async_computation.7 | async-start | bytes 4718592 | tf_op jit(solution)/shard_map/all_gather | solution.py:78
  857.7 557.4 %all-gather.20.cloned.1.call-start = ((), (), s32[]{:S(2)}) async-start(), calls=%async_computation.8 | async-start | bytes 4718592 | tf_op jit(solution)/shard_map/all_gather | solution.py:79
  915.1 33.5 %copy-start.4 = (s32[1,512,8]{2,1,0:T(8,128)S(1)}, s32[1,512,8]{2,1,0:T(8,128)}, u32[]{:S(2)}) copy-start(s32[1,512,8]{2,1,0:T(8,128)} %copy-done.3) | copy-start | bytes 49156
  1300.3 95.9 %copy-start.10 = (f32[512,8]{1,0:T(8,128)S(1)}, f32[512,8]{1,0:T(8,128)}, u32[]{:S(2)}) copy-start(f32[512,8]{1,0:T(8,128)} %fusion.44) | copy-start | bytes 49156
  (3 other events, 14.6 us)
Sparse Core Ops, SparseCore 0:
  9.0 50.9 all-gather.9
  61.6 46.6 all-gather.11
  109.9 46.6 all-gather.7
  158.0 46.6 all-gather.13
  858.5 64.5 all-gather.15
  924.6 61.3 all-gather.17
  987.6 44.9 all-gather.19
where the time goes:
time: 1440 us; the launch traced here: 1430 us
  waiting for transfers between devices  380 us (26%)
  blocking collectives  375 us (26%)
  local copies, waits for them, and re-layouts  304 us (21%)
  matrix products  207 us (14%)
  other arithmetic  145 us (10%)
    all_to_all x1, blocking collectives, local_layer(): lax.all_to_all(send_buf, 'ep', 0, 2, tiled=True)  375 us
    all_to_all x1, waiting for transfers between devices, local_layer(): lax.all_to_all(expert_out.reshape(1, local_experts, group * capacity, d_m...  314 us
    gather x1, local copies, waits for them, and re-layouts, local_layer(): jnp.take(returned.reshape(n_experts * capacity, d_model), slot_of_assign,...  95.9 us
    dot_general x1, matrix products, local_layer(): jnp.einsum('ecd,edf->ecf', received, up_loc, preferred_element_type=jnp.f...  53.8 us
    gather x1, local copies, waits for them, and re-layouts, slot_plan(): slot_token = jnp.take(sort_order, slot_rows.reshape(-1)) // top_k  45.5 us
    dot_general x1, matrix products, local_layer(): jnp.einsum('ecd,edf->ecf', received, gate_loc, preferred_element_type=jnp...  44.3 us
    dot_general x1, matrix products, local_layer(): jnp.einsum('ecf,efd->ecd', middle, down_loc, preferred_element_type=jnp.f...  43.4 us
    gather x1, local copies, waits for them, and re-layouts, local_layer(): jnp.take(moe_in, slot_token, axis=0)  40.5 us
  transfers between devices with their start and end apart: 8, of which 4 were waited for; matrix products, arithmetic and copies ran while one was open for 26% of the time, Pallas kernels for 0%

commit v1 on v0

v1 whole, which is shorter than its diff:
```python
import functools
import jax
import jax.numpy as jnp
from jax import lax
from jax.experimental import pallas as pl
from jax.experimental.pallas import tpu as pltpu
from jax.sharding import PartitionSpec as P

EPSILON = 1e-6
CAP_FACTOR = 2
VMEM_BYTES = 60 * 1024 * 1024


def rms_norm(values):
    as_f32 = values.astype(jnp.float32)
    return as_f32 * lax.rsqrt(jnp.mean(as_f32 * as_f32, axis=-1, keepdims=True) + EPSILON)


def params(**kw):
    return pltpu.CompilerParams(vmem_limit_bytes=VMEM_BYTES, **kw)


def attention_kernel(q_ref, k_ref, v_ref, o_ref, *, parts):
    seq, head = q_ref.shape
    step = seq // parts
    for part in range(parts):
        lo, hi = part * step, (part + 1) * step
        scores = lax.dot_general(q_ref[lo:hi, :], k_ref[:hi, :], (((1,), (1,)), ((), ())), preferred_element_type=jnp.float32) * (head ** -0.5)
        rows = lo + lax.broadcasted_iota(jnp.int32, scores.shape, 0)
        cols = lax.broadcasted_iota(jnp.int32, scores.shape, 1)
        scores = jnp.where(rows >= cols, scores, -1e30)
        weights = jnp.exp(scores - jnp.max(scores, axis=-1, keepdims=True))
        probs = (weights / jnp.sum(weights, axis=-1, keepdims=True)).astype(jnp.bfloat16)
        o_ref[lo:hi, :] = jnp.dot(probs, v_ref[:hi, :], preferred_element_type=jnp.float32).astype(jnp.bfloat16)


def attention(queries, keys, vals, head):
    seq, width = queries.shape
    spec = pl.BlockSpec((seq, head), lambda i: (0, i))
    return pl.pallas_call(
        functools.partial(attention_kernel, parts=2),
        grid=(width // head,),
        in_specs=[spec] * 3,
        out_specs=spec,
        out_shape=jax.ShapeDtypeStruct((seq, width), jnp.bfloat16),
        compiler_params=params(),
        cost_estimate=pl.CostEstimate(flops=8 * seq * seq * width, bytes_accessed=8 * seq * width, transcendentals=0),
        name="attention",
    )(queries, keys, vals)


def dispatch_kernel(rank_ref, u_ref, x_ref, *, capacity):
    local = rank_ref.shape[1]
    n_tok = u_ref.shape[1]
    picks = []
    slots = lax.broadcasted_iota(jnp.int32, (capacity, n_tok), 0)
    for e in range(local):
        picks.append((rank_ref[0, e:e + 1, :] == slots).astype(jnp.float32).astype(jnp.bfloat16))
    pick = jnp.concatenate(picks, axis=0)
    width = 512
    for c in range(u_ref.shape[2] // width):
        cols = slice(c * width, (c + 1) * width)
        rows = jnp.dot(pick, u_ref[0, :, cols], preferred_element_type=jnp.float32).astype(jnp.bfloat16)
        for e in range(local):
            x_ref[e, 0, :, cols] = rows[e * capacity:(e + 1) * capacity, :]


def dispatch(rank, tokens, capacity):
    n_src, local, n_tok = rank.shape
    d_model = tokens.shape[2]
    return pl.pallas_call(
        functools.partial(dispatch_kernel, capacity=capacity),
        grid=(n_src,),
        in_specs=[pl.BlockSpec((1, local, n_tok), lambda s: (s, 0, 0)), pl.BlockSpec((1, n_tok, d_model), lambda s: (s, 0, 0))],
        out_specs=pl.BlockSpec((local, 1, capacity, d_model), lambda s: (0, s, 0, 0)),
        out_shape=jax.ShapeDtypeStruct((local, n_src, capacity, d_model), jnp.bfloat16),
        compiler_params=params(),
        cost_estimate=pl.CostEstimate(flops=2 * n_src * local * capacity * n_tok * d_model, bytes_accessed=4 * n_src * local * capacity * d_model, transcendentals=0),
        name="dispatch",
    )(rank, tokens)


def expert_kernel(x_ref, gate_ref, up_ref, down_ref, f_ref, *, chunk):
    n_rows = x_ref.shape[1]

    @pl.loop(0, n_rows // chunk)
    def _(i):
        rows = pl.ds(pl.multiple_of(i * chunk, chunk), chunk)
        x = x_ref[0, rows, :]
        gate_act = jnp.dot(x, gate_ref[0], preferred_element_type=jnp.float32)
        up_act = jnp.dot(x, up_ref[0], preferred_element_type=jnp.float32)
        middle = (gate_act * jax.nn.sigmoid(gate_act) * up_act).astype(jnp.bfloat16)
        f_ref[0, rows, :] = jnp.dot(middle, down_ref[0], preferred_element_type=jnp.float32).astype(jnp.bfloat16)


def experts(rows, gate_w, up_w, down_w):
    local, n_rows, d_model = rows.shape
    width = gate_w.shape[2]
    return pl.pallas_call(
        functools.partial(expert_kernel, chunk=256),
        grid=(local,),
        in_specs=[
            pl.BlockSpec((1, n_rows, d_model), lambda e: (e, 0, 0)),
            pl.BlockSpec((1, d_model, width), lambda e: (e, 0, 0)),
            pl.BlockSpec((1, d_model, width), lambda e: (e, 0, 0)),
            pl.BlockSpec((1, width, d_model), lambda e: (e, 0, 0)),
        ],
        out_specs=pl.BlockSpec((1, n_rows, d_model), lambda e: (e, 0, 0)),
        out_shape=jax.ShapeDtypeStruct(rows.shape, jnp.bfloat16),
        compiler_params=params(),
        cost_estimate=pl.CostEstimate(flops=6 * local * n_rows * d_model * width, bytes_accessed=6 * local * d_model * width, transcendentals=0),
        name="experts",
    )(rows, gate_w, up_w, down_w)


def combine_kernel(rank_ref, piece_ref, f_ref, out_ref):
    n_tok, local = rank_ref.shape[1:]
    capacity = f_ref.shape[2]
    pieces = piece_ref.shape[2] // local
    slots = lax.broadcasted_iota(jnp.int32, (n_tok, capacity), 1)
    rank = rank_ref[0]
    weights = piece_ref[0]
    rows = [[] for _ in range(pieces)]
    for e in range(local):
        hit = rank[:, e:e + 1] == slots
        for k in range(pieces):
            column = k * local + e
            rows[k].append(jnp.where(hit, weights[:, column:column + 1], 0.0).astype(jnp.bfloat16))
    spread = [jnp.concatenate(r, axis=1) for r in rows]
    width = 512
    for c in range(out_ref.shape[2] // width):
        cols = slice(c * width, (c + 1) * width)
        data = jnp.concatenate([f_ref[e, 0, :, cols] for e in range(local)], axis=0)
        total = jnp.dot(spread[0], data, preferred_element_type=jnp.float32)
        for k in range(1, pieces):
            total += jnp.dot(spread[k], data, preferred_element_type=jnp.float32)
        out_ref[0, :, cols] = total


def combine(rank_t, pieces, results):
    local, n_src, capacity, d_model = results.shape
    n_tok = rank_t.shape[1]
    width = pieces.shape[2]
    return pl.pallas_call(
        combine_kernel,
        grid=(n_src,),
        in_specs=[
            pl.BlockSpec((1, n_tok, local), lambda s: (s, 0, 0)),
            pl.BlockSpec((1, n_tok, width), lambda s: (s, 0, 0)),
            pl.BlockSpec((local, 1, capacity, d_model), lambda s: (0, s, 0, 0)),
        ],
        out_specs=pl.BlockSpec((1, n_tok, d_model), lambda s: (s, 0, 0)),
        out_shape=jax.ShapeDtypeStruct((n_src, n_tok, d_model), jnp.float32),
        compiler_params=params(),
        cost_estimate=pl.CostEstimate(flops=6 * n_src * local * capacity * n_tok * d_model, bytes_accessed=8 * n_src * local * capacity * d_model, transcendentals=0),
        name="combine",
    )(rank_t, pieces, results)


def bf16_pieces(values):
    first = lax.reduce_precision(values, 8, 7)
    second = lax.reduce_precision(values - first, 8, 7)
    third = values - first - second
    return first, second, third


def local_layer(x_loc, q_shard, k_shard, v_shard, o_shard, w_router, gate_loc, up_loc, down_loc, sgate_shard, sup_shard, sdown_shard, ids_loc, group):
    n_seq, seq_len, d_model = x_loc.shape
    heads, head = q_shard.shape[1:]
    n_tok = n_seq * seq_len
    top_k = ids_loc.shape[-1]
    local = gate_loc.shape[0]
    n_experts = local * group
    capacity = CAP_FACTOR * n_tok * top_k // n_experts

    def gathered(shard):
        return lax.all_gather(shard.reshape(shard.shape[0], -1), 'ep', axis=0, tiled=True)

    def project(rows, weight):
        return jnp.dot(rows, weight, preferred_element_type=jnp.float32).astype(jnp.bfloat16)

    ids_all = lax.all_gather(ids_loc.reshape(n_tok, top_k).T, 'ep', axis=0)
    mine = lax.axis_index('ep') * local + jnp.arange(local)
    chosen = ids_all[:, None, :, :] == mine[None, :, None, None]
    member = jnp.any(chosen, axis=2)
    before = (jnp.arange(n_tok)[:, None] < jnp.arange(n_tok)[None, :]).astype(jnp.bfloat16)
    rank = jnp.einsum('set,tq->seq', member.astype(jnp.bfloat16), before, preferred_element_type=jnp.float32).astype(jnp.int32)
    rank = jnp.where(member, rank, -1)

    x_flat = x_loc.reshape(n_tok, d_model)
    normed = rms_norm(x_flat).astype(jnp.bfloat16)
    queries = project(normed, gathered(q_shard))
    keys_all = project(normed, gathered(k_shard))
    vals_all = project(normed, gathered(v_shard))
    attended = [attention(queries[i * seq_len:(i + 1) * seq_len], keys_all[i * seq_len:(i + 1) * seq_len], vals_all[i * seq_len:(i + 1) * seq_len], head) for i in range(n_seq)]
    attended = attended[0] if n_seq == 1 else jnp.concatenate(attended, axis=0)
    attn_out = project(attended, gathered(o_shard))
    residual = (x_flat.astype(jnp.float32) + attn_out.astype(jnp.float32)).astype(jnp.bfloat16)

    hidden = rms_norm(residual)
    moe_in = hidden.astype(jnp.bfloat16)
    tokens = lax.all_gather(moe_in, 'ep', axis=0)
    logits = jnp.dot(hidden, w_router, precision=lax.Precision.HIGHEST, preferred_element_type=jnp.float32)
    tok_ids = ids_loc.reshape(n_tok, top_k)
    picked = tok_ids[:, :, None] == jnp.arange(n_experts)[None, None, :]
    chosen_logits = jnp.sum(jnp.where(picked, logits[:, None, :], 0.0), axis=2)
    gate_probs = jax.nn.softmax(chosen_logits, axis=-1)
    gates_all = lax.all_gather(gate_probs.T, 'ep', axis=0)
    weight = jnp.sum(jnp.where(chosen, gates_all[:, None, :, :], 0.0), axis=2)
    pieces = jnp.concatenate(bf16_pieces(weight), axis=1).transpose(0, 2, 1)

    rows = dispatch(rank, tokens, capacity)
    results = experts(rows.reshape(local, group * capacity, d_model), gate_loc, up_loc, down_loc)
    partial = combine(rank.transpose(0, 2, 1), pieces, results.reshape(local, group, capacity, d_model))
    routed = lax.psum_scatter(partial.reshape(group * n_tok, d_model), 'ep', scatter_dimension=0, tiled=True)

    gate_act = jnp.dot(moe_in, gathered(sgate_shard), preferred_element_type=jnp.float32)
    up_act = jnp.dot(moe_in, gathered(sup_shard), preferred_element_type=jnp.float32)
    middle = (jax.nn.silu(gate_act) * up_act).astype(jnp.bfloat16)
    shared = project(middle, gathered(sdown_shard))
    y_out = (residual.astype(jnp.float32) + routed + shared.astype(jnp.float32)).astype(jnp.bfloat16)
    return y_out.reshape(n_seq, seq_len, d_model)


def solution(mesh):
    tok_spec = P(('dp', 'ep'), None, None)
    row_spec = P('ep', None)
    cube_spec = P('ep', None, None)
    in_specs = (tok_spec, cube_spec, cube_spec, cube_spec, row_spec, P(None, None), cube_spec, cube_spec, cube_spec, row_spec, row_spec, row_spec, tok_spec)
    return jax.shard_map(functools.partial(local_layer, group=mesh.shape['ep']), mesh=mesh, in_specs=in_specs, out_specs=tok_spec, check_vma=False)
```

time: 1440 us -> 693 us (0.48)
  blocking collectives: 375 us -> 26.4 us
  local copies, waits for them, and re-layouts: 304 us -> 14.7 us
  Pallas kernels: 0 us -> 226 us
  matrix products: 207 us -> 60.6 us
  other arithmetic: 145 us -> 3.51 us
  waiting for transfers between devices: 380 us -> 347 us
    all_to_all x1 -> x0, blocking collectives: 375 us -> none  [local_layer(): lax.all_to_all(send_buf, 'ep', 0, 2, tiled=True)]
    all_to_all x1 -> x0, waiting for transfers between devices: 314 us -> none  [local_layer(): lax.all_to_all(expert_out.reshape(1, local_experts, group * capacity, d_m...]
    pallas_call x0 -> x4, Pallas kernels: none -> 226 us  [the longest x1 118 us: experts(): pl.pallas_call(functools.partial(expert_kernel, chunk=256), grid=(local,)...]
    gather x11 -> x0, local copies, waits for them, and re-layouts: 218 us -> none  [the longest x1 95.9 us: local_layer(): jnp.take(returned.reshape(n_experts * capacity, d_model), slot_of_assign,...]
    reduce_scatter x0 -> x1, waiting for transfers between devices: none -> 160 us  [local_layer(): lax.psum_scatter(partial.reshape(group * n_tok, d_model), 'ep', scatter_d...]
    dot_general x9 -> x7, matrix products: 202 us -> 56.1 us  [the longest x5 48.1 us: project(): jnp.dot(rows, weight, preferred_element_type=jnp.float32)]
    all_gather x7 -> x8, waiting for transfers between devices: 60.9 us -> 184 us  [the longest x7 143 us: gathered(): lax.all_gather(shard.reshape(shard.shape[0], -1), 'ep', axis=0, tiled=True)]
    all_to_all x2 -> x0, local copies, waits for them, and re-layouts: 52.9 us -> none  [the longest x1 30 us: local_layer(): lax.all_to_all(expert_out.reshape(1, local_experts, group * capacity, d_m...]
  transfers between devices with their start and end apart: 8 -> 9, of which waited for: 4 -> 6; matrix products, arithmetic and copies ran while one was open for 26% -> 8% of each run, Pallas kernels for 0% -> 33%
where the time goes in v1:
time: 693 us; the launch traced here: 692 us
  waiting for transfers between devices  347 us (50%)
  Pallas kernels  226 us (33%)
  matrix products  60.6 us (9%)
  blocking collectives  26.4 us (4%)
  local copies, waits for them, and re-layouts  14.7 us (2%)
  between operations  13.4 us (2%)
    reduce_scatter x1, waiting for transfers between devices, local_layer(): lax.psum_scatter(partial.reshape(group * n_tok, d_model), 'ep', scatter_d...  160 us
    all_gather x7, waiting for transfers between devices, gathered(): lax.all_gather(shard.reshape(shard.shape[0], -1), 'ep', axis=0, tiled=True)  143 us
    pallas_call x1, Pallas kernels, experts(): pl.pallas_call(functools.partial(expert_kernel, chunk=256), grid=(local,)...  118 us
    pallas_call x1, Pallas kernels, combine(): pl.pallas_call(combine_kernel, grid=(n_src,), in_specs=[pl.BlockSpec((1,...  64.4 us
    dot_general x5, matrix products, project(): jnp.dot(rows, weight, preferred_element_type=jnp.float32)  48.1 us
    all_gather x1, waiting for transfers between devices, local_layer(): tokens = lax.all_gather(moe_in, 'ep', axis=0)  41 us
    pallas_call x1, Pallas kernels, dispatch(): pl.pallas_call(functools.partial(dispatch_kernel, capacity=capacity), gri...  25.2 us
    pallas_call x1, Pallas kernels, attention(): pl.pallas_call(functools.partial(attention_kernel, parts=2), grid=(width...  18.3 us
  transfers between devices with their start and end apart: 9, of which 6 were waited for; matrix products, arithmetic and copies ran while one was open for 8% of the time, Pallas kernels for 33%

profile of v1, /device:TPU:81, one launch (start us, length us, event | category | flops | bytes accessed | tf_op | source)
XLA Modules:
  0.0 691.7 jit_solution(6837461329417376308)
XLA Ops:
  6.6 2.6 copy.36
  9.2 2.6 copy.37
  12.0 2.5 copy.38
  15.7 44.6 %all-gather.16.cloned.1.call-done = bf16[2048,2048]{1,0:T(8,128)(2,1)} async-done(((bf16[256,2048]{1,0:T(8,128)(2,1)}), bf16[2048,2048]{1,0:T(8,128)(2,1)}) %all-gather.16.cloned.1.call-update) | async-done | bytes 8388624 | tf_op jit(solution)/shard_map/all_gather | solution.py:177
  60.3 9.2 %convolution_convert_fusion.2.v_ref = bf16[512,2048]{1,0:T(8,128)(2,1)} fusion(bf16[2048,2048]{1,0:T(8,128)(2,1)} %all-gather.16.cloned.1.call-done, bf16[1,512,2048]{2,1,0:T(8,128)(2,1)S(1)} %copy-done.4, f32[512]{0:T(512)S(1)} %add_rsqrt_fusion.1), kind=kOutput, calls=%fused_computation.16 | convolution fusion | flops 4299161600 | bytes 12584960 | tf_op jit(solution)/shard_map/dot_general | solution.py:180
  69.5 39.0 %all-gather.14.cloned.1.call-done = bf16[2048,2048]{1,0:T(8,128)(2,1)} async-done(((bf16[256,2048]{1,0:T(8,128)(2,1)}), bf16[2048,2048]{1,0:T(8,128)(2,1)}) %all-gather.14.cloned.1.call-update) | async-done | bytes 8388624 | tf_op jit(solution)/shard_map/all_gather | solution.py:177
  108.6 9.2 %convolution_convert_fusion.3.k_ref = bf16[512,2048]{1,0:T(8,128)(2,1)} fusion(bf16[2048,2048]{1,0:T(8,128)(2,1)} %all-gather.14.cloned.1.call-done, bf16[1,512,2048]{2,1,0:T(8,128)(2,1)S(1)} %copy-done.4, f32[512]{0:T(512)S(1)} %add_rsqrt_fusion.1), kind=kOutput, calls=%fused_computation.17 | convolution fusion | flops 4299161600 | bytes 12584960 | tf_op jit(solution)/shard_map/dot_general | solution.py:180
  117.8 39.1 %all-gather.12.cloned.1.call-done = bf16[2048,2048]{1,0:T(8,128)(2,1)} async-done(((bf16[256,2048]{1,0:T(8,128)(2,1)}), bf16[2048,2048]{1,0:T(8,128)(2,1)}) %all-gather.12.cloned.1.call-update) | async-done | bytes 8388624 | tf_op jit(solution)/shard_map/all_gather | solution.py:177
  156.9 9.2 %convolution_convert_fusion.4.q_ref = bf16[512,2048]{1,0:T(8,128)(2,1)} fusion(bf16[2048,2048]{1,0:T(8,128)(2,1)} %all-gather.12.cloned.1.call-done, bf16[1,512,2048]{2,1,0:T(8,128)(2,1)S(1)} %copy-done.4, f32[512]{0:T(512)S(1)} %add_rsqrt_fusion.1), kind=kOutput, calls=%fused_computation.18 | convolution fusion | flops 4299161600 | bytes 12584960 | tf_op jit(solution)/shard_map/dot_general | solution.py:180
  166.1 18.3 %attention.1 = bf16[512,2048]{1,0:T(8,128)(2,1)} custom-call(bf16[512,2048]{1,0:T(8,128)(2,1)} %convolution_convert_fusion.4.q_ref, bf16[512,2048]{1,0:T(8,128)(2,1)} %convolution_convert_fusion.3.k_ref, bf16[512,2048]{1,0:T(8,128)(2,1)} %convolution_convert_fusion.2.v_ref), custom_call_target="tpu_custom_call" | custom-call | flops 4294967296 | bytes 8388608 | tf_op jit(solution)/shard_map/attention/pallas_call | solution.py:40
  184.3 20.7 %all-gather.18.cloned.1.call-done = bf16[2048,2048]{1,0:T(8,128)(2,1)} async-done(((bf16[256,2048]{1,0:T(8,128)(2,1)}), bf16[2048,2048]{1,0:T(8,128)(2,1)}) %all-gather.18.cloned.1.call-update) | async-done | bytes 8388624 | tf_op jit(solution)/shard_map/all_gather | solution.py:177
  205.0 9.3 %fusion.2 = (f32[512]{0:T(512)S(1)}, bf16[512,2048]{1,0:T(8,128)(2,1)S(1)}) fusion(bf16[512,2048]{1,0:T(8,128)(2,1)} %attention.1, bf16[2048,2048]{1,0:T(8,128)(2,1)} %all-gather.18.cloned.1.call-done, bf16[1,512,2048]{2,1,0:T(8,128)(2,1)} %param.13), kind=kOutput, calls=%fused_computation.8 | convolution fusion | flops 4303355392 | bytes 14682112 | tf_op jit(solution)/shard_map/dot_general | solution.py:180
  218.7 13.1 %all-gather = s32[64,512]{1,0:T(8,128)S(1)} all-gather(s32[8,512]{1,0:T(8,128)S(1)} %bitcast.60), channel_id=2, replica_groups=mesh['dp'=4,'ep'=8] {'ep'}, dimensions={0}, use_global_device_ids=true | all-gather | bytes 147456 | tf_op jit(solution)/shard_map/all_gather | solution.py:182
  233.1 2.2 convert_select_fusion
  235.2 2.8 copy.28.rank_ref
  238.1 4.4 fusion.1
  242.7 13.3 %all-gather.1 = f32[64,512]{1,0:T(8,128)S(1)} all-gather(f32[8,512]{1,0:T(8,128)S(1)} %divide_bitcast_fusion), channel_id=3, replica_groups=mesh['dp'=4,'ep'=8] {'ep'}, dimensions={0}, use_global_device_ids=true | all-gather | bytes 147456 | tf_op jit(solution)/shard_map/all_gather | solution.py:208
  258.4 41.0 %all-gather.26.cloned.1.call-done = bf16[4096,2048]{1,0:T(8,128)(2,1)} async-done(((bf16[512,2048]{1,0:T(8,128)(2,1)}), bf16[4096,2048]{1,0:T(8,128)(2,1)}) %all-gather.26.cloned.1.call-update) | async-done | bytes 16777232 | tf_op jit(solution)/shard_map/all_gather | solution.py:202
  299.4 25.2 %dispatch.1 = bf16[8,8,128,2048]{3,2,1,0:T(8,128)(2,1)} custom-call(s32[8,8,512]{2,1,0:T(8,128)} %copy.28.rank_ref, bf16[8,512,2048]{2,1,0:T(8,128)(2,1)} %bitcast.62), custom_call_target="tpu_custom_call" | custom-call | flops 17179869184 | bytes 67108864 | tf_op jit(solution)/shard_map/dispatch/pallas_call | solution.py:71
  324.6 117.6 %experts.1 = bf16[8,1024,2048]{2,1,0:T(8,128)(2,1)} custom-call(bf16[8,1024,2048]{2,1,0:T(8,128)(2,1)} %bitcast.64, bf16[8,2048,1024]{2,1,0:T(8,128)(2,1)} %gate_ref.1, bf16[8,2048,1024]{2,1,0:T(8,128)(2,1)} %up_ref.1, bf16[8,1024,2048]{2,1,0:T(8,128)(2,1)} %down_ref.1), custom_call_target="tpu_custom_call" | custom-call | flops 103079215104 | bytes 100663296 | tf_op jit(solution)/shard_map/experts/pallas_call | solution.py:99
  442.3 64.4 %combine.1 = f32[8,512,2048]{2,1,0:T(8,128)} custom-call(s32[8,512,8]{2,1,0:T(8,128)} %bitcast.53, f32[8,512,24]{2,1,0:T(8,128)} %bitcast.52, bf16[8,8,128,2048]{3,2,1,0:T(8,128)(2,1)} %bitcast.63), custom_call_target="tpu_custom_call" | custom-call | flops 51539607552 | bytes 134217728 | tf_op jit(solution)/shard_map/combine/pallas_call | solution.py:144
  508.3 5.9 fusion.21
  514.2 159.8 %reduce-scatter.2.cloned.1.call-done = f32[512,2048]{1,0:T(8,128)} async-done(((f32[4096,2048]{1,0:T(8,128)}), f32[512,2048]{1,0:T(8,128)}) %reduce-scatter.2.cloned.1.call-update) | async-done | bytes 4194320 | tf_op jit(solution)/shard_map/reduce_scatter | solution.py:215
  674.0 11.2 %fusion.8 = bf16[1,512,2048]{2,1,0:T(8,128)(2,1)} fusion(bf16[1024,2048]{1,0:T(8,128)(2,1)} %all-gather.24.cloned.1.call-done, f32[512,2048]{1,0:T(8,128)} %reduce-scatter.2.cloned.1.call-done, bf16[512,2048]{1,0:T(8,128)(2,1)S(1)} %copy-done.3, f32[512,1024]{1,0:T(8,128)} %fusion.21, bf16[2048,1024]{1,0:T(8,128)(2,1)} %all-gather.22.cloned.1.call-done, ...), kind=kOutput, calls=%fused_computation.19 | convolution fusion | flops 4307550208 | bytes 18876416 | tf_op jit(solution)/shard_map/dot_general | solution.py:180
  (52 shorter events, 11.1 us)
Async XLA Ops:
  6.5 231.5 %copy-start = (f32[2048,64]{0,1:T(8,128)S(1)}, f32[2048,64]{0,1:T(8,128)}, u32[]{:S(2)}) copy-start(f32[2048,64]{0,1:T(8,128)} %param.18) | copy-start | bytes 1572868
  6.6 53.7 %all-gather.16.cloned.1.call-start = ((), (), s32[]{:S(2)}) async-start(), calls=%async_computation.3 | async-start | bytes 9437184 | tf_op jit(solution)/shard_map/all_gather | solution.py:177
  9.1 6.1 copy-start.4
  9.2 99.4 %all-gather.14.cloned.1.call-start = ((), (), s32[]{:S(2)}) async-start(), calls=%async_computation.2 | async-start | bytes 9437184 | tf_op jit(solution)/shard_map/all_gather | solution.py:177
  11.9 145.0 %all-gather.12.cloned.1.call-start = ((), (), s32[]{:S(2)}) async-start(), calls=%async_computation.1 | async-start | bytes 9437184 | tf_op jit(solution)/shard_map/all_gather | solution.py:177
  14.5 190.5 %all-gather.18.cloned.1.call-start = ((), (), s32[]{:S(2)}) async-start(), calls=%async_computation.4 | async-start | bytes 9437184 | tf_op jit(solution)/shard_map/all_gather | solution.py:177
  15.1 284.3 %all-gather.26.cloned.1.call-start = ((), (), s32[]{:S(2)}) async-start(), calls=%async_computation.9 | async-start | bytes 18874368 | tf_op jit(solution)/shard_map/all_gather | solution.py:202
  214.3 23.8 %copy-start.2 = (bf16[512,2048]{1,0:T(8,128)(2,1)}, bf16[512,2048]{1,0:T(8,128)(2,1)S(1)}, u32[]{:S(2)}) copy-start(bf16[512,2048]{1,0:T(8,128)(2,1)S(1)} %get-tuple-element.9) | copy-start | bytes 6291460
  214.3 4.4 copy-start.5
  214.3 23.7 %copy-start.6 = (f32[512]{0:T(512)}, f32[512]{0:T(512)S(1)}, u32[]{:S(2)}) copy-start(f32[512]{0:T(512)S(1)} %add_rsqrt_fusion) | copy-start | bytes 6148
  216.4 290.4 %all-gather.20.cloned.1.call-start = ((), (), s32[]{:S(2)}) async-start(), calls=%async_computation.6 | async-start | bytes 4718592 | tf_op jit(solution)/shard_map/all_gather | solution.py:177
  217.0 297.1 %all-gather.22.cloned.1.call-start = ((), (), s32[]{:S(2)}) async-start(), calls=%async_computation.7 | async-start | bytes 4718592 | tf_op jit(solution)/shard_map/all_gather | solution.py:177
  217.8 296.3 %all-gather.24.cloned.1.call-start = ((), (), s32[]{:S(2)}) async-start(), calls=%async_computation.8 | async-start | bytes 4718592 | tf_op jit(solution)/shard_map/all_gather | solution.py:177
  218.6 455.4 %reduce-scatter.2.cloned.1.call-start = ((), (), s32[]{:S(2)}) async-start(), calls=%async_computation.5 | async-start | bytes 37748736 | tf_op jit(solution)/shard_map/reduce_scatter | solution.py:215
  506.7 1.6 copy-start.3
  506.7 1.6 copy-start.7
  674.0 11.2 %copy-start.1 = (f32[2048,64]{0,1:T(8,128)S(1)}, f32[2048,64]{0,1:T(8,128)}, u32[]{:S(2)}) copy-start(f32[2048,64]{0,1:T(8,128)} %param.18) | copy-start | bytes 1572868
Sparse Core Ops, SparseCore 0:
  9.3 50.9 all-gather.15
  61.9 46.6 all-gather.13
  110.2 46.6 all-gather.11
  158.3 46.6 all-gather.17
  216.5 82.8 all-gather.25
  300.9 29.2 all-gather.19
  331.8 28.6 all-gather.21
  362.1 28.6 all-gather.23
  506.9 167.0 reduce-scatter.1

commit v2 on v1

v2 whole, which is shorter than its diff:
```python
import functools
import jax
import jax.numpy as jnp
from jax import lax
from jax.experimental import pallas as pl
from jax.experimental.pallas import tpu as pltpu
from jax.sharding import PartitionSpec as P

EPSILON = 1e-6
CAP_FACTOR = 2
ALIGN = 16
VMEM_BYTES = 60 * 1024 * 1024
MAX_VMEM = 67043328


def rms_norm(values):
    as_f32 = values.astype(jnp.float32)
    return as_f32 * lax.rsqrt(jnp.mean(as_f32 * as_f32, axis=-1, keepdims=True) + EPSILON)


def params(**kw):
    return pltpu.CompilerParams(vmem_limit_bytes=VMEM_BYTES, **kw)


def attention_kernel(q_ref, k_ref, v_ref, o_ref, *, parts):
    seq, head = q_ref.shape
    step = seq // parts
    for part in range(parts):
        lo, hi = part * step, (part + 1) * step
        scores = lax.dot_general(q_ref[lo:hi, :], k_ref[:hi, :], (((1,), (1,)), ((), ())), preferred_element_type=jnp.float32) * (head ** -0.5)
        rows = lo + lax.broadcasted_iota(jnp.int32, scores.shape, 0)
        cols = lax.broadcasted_iota(jnp.int32, scores.shape, 1)
        scores = jnp.where(rows >= cols, scores, -1e30)
        weights = jnp.exp(scores - jnp.max(scores, axis=-1, keepdims=True))
        probs = (weights / jnp.sum(weights, axis=-1, keepdims=True)).astype(jnp.bfloat16)
        o_ref[lo:hi, :] = jnp.dot(probs, v_ref[:hi, :], preferred_element_type=jnp.float32).astype(jnp.bfloat16)


def attention(queries, keys, vals, head):
    seq, width = queries.shape
    spec = pl.BlockSpec((seq, head), lambda i: (0, i))
    return pl.pallas_call(
        functools.partial(attention_kernel, parts=2),
        grid=(width // head,),
        in_specs=[spec] * 3,
        out_specs=spec,
        out_shape=jax.ShapeDtypeStruct((seq, width), jnp.bfloat16),
        compiler_params=params(),
        cost_estimate=pl.CostEstimate(flops=8 * seq * seq * width, bytes_accessed=8 * seq * width, transcendentals=0),
        name="attention",
    )(queries, keys, vals)


def dispatch_kernel(order_ref, rank_ref, u_ref, x_ref, *, capacity):
    local, n_tok = rank_ref.shape[1:]
    slots = lax.broadcasted_iota(jnp.int32, (capacity, n_tok), 0)
    picks = [(rank_ref[0, e:e + 1, :] == slots).astype(jnp.float32).astype(jnp.bfloat16) for e in range(local)]
    pick = jnp.concatenate(picks, axis=0)
    width = 512
    for c in range(u_ref.shape[2] // width):
        cols = slice(c * width, (c + 1) * width)
        rows = jnp.dot(pick, u_ref[0, :, cols], preferred_element_type=jnp.float32).astype(jnp.bfloat16)
        for e in range(local):
            x_ref[0, e, :, cols] = rows[e * capacity:(e + 1) * capacity, :]


def dispatch(order, rank, tokens, capacity):
    n_src, local, n_tok = rank.shape
    d_model = tokens.shape[2]
    return pl.pallas_call(
        functools.partial(dispatch_kernel, capacity=capacity),
        grid_spec=pltpu.PrefetchScalarGridSpec(
            num_scalar_prefetch=1,
            grid=(n_src,),
            in_specs=[pl.BlockSpec((1, local, n_tok), lambda s, order: (s, 0, 0)), pl.BlockSpec((1, n_tok, d_model), lambda s, order: (order[s], 0, 0))],
            out_specs=pl.BlockSpec((1, local, capacity, d_model), lambda s, order: (s, 0, 0, 0)),
        ),
        out_shape=jax.ShapeDtypeStruct((n_src, local, capacity, d_model), jnp.bfloat16),
        compiler_params=params(),
        cost_estimate=pl.CostEstimate(flops=2 * n_src * local * capacity * n_tok * d_model, bytes_accessed=4 * n_src * local * capacity * d_model, transcendentals=0),
        name="dispatch",
    )(order, rank, tokens)


def expert_kernel(size_ref, start_ref, total_ref, x_ref, gate_ref, up_ref, down_ref, f_ref, x_buf, f_buf, in_sems, out_sems, *, chunk):
    n_src, _, capacity, d_model = x_ref.shape
    e, local = pl.program_id(0), pl.num_programs(0)
    slot = lax.rem(e, 2)
    zeros = jnp.zeros((capacity, d_model), jnp.bfloat16)

    def fetch(r, expert, where):
        size = pl.multiple_of(size_ref[r, expert], ALIGN)
        start = pl.multiple_of(start_ref[r, expert], ALIGN)
        return pltpu.make_async_copy(x_ref.at[r, expert, pl.ds(0, size), :], x_buf.at[where, pl.ds(start, size), :], in_sems.at[where, r])

    def put(r, expert, where):
        start = pl.multiple_of(start_ref[r, expert], ALIGN)
        return pltpu.make_async_copy(f_buf.at[where, pl.ds(start, capacity), :], f_ref.at[r, expert], out_sems.at[where, r])

    @pl.when(e == 0)
    def _():
        for r in range(n_src):
            fetch(r, 0, 0).start()

    @pl.when(e + 1 < local)
    def _():
        for r in range(n_src):
            fetch(r, e + 1, 1 - slot).start()

    for r in range(n_src):
        fetch(r, e, slot).wait()

    @pl.when(e >= 2)
    def _():
        for r in range(n_src):
            put(r, e - 2, slot).wait()

    total = total_ref[e]
    x_buf[slot, pl.ds(pl.multiple_of(total, ALIGN), capacity), :] = zeros
    chunks = (total + chunk - 1) // chunk

    @pl.loop(0, chunks)
    def _(i):
        rows = pl.ds(pl.multiple_of(i * chunk, chunk), chunk)
        x = x_buf[slot, rows, :]
        gate_act = jnp.dot(x, gate_ref[0], preferred_element_type=jnp.float32)
        up_act = jnp.dot(x, up_ref[0], preferred_element_type=jnp.float32)
        middle = (gate_act * jax.nn.sigmoid(gate_act) * up_act).astype(jnp.bfloat16)
        f_buf[slot, rows, :] = jnp.dot(middle, down_ref[0], preferred_element_type=jnp.float32).astype(jnp.bfloat16)

    f_buf[slot, pl.ds(pl.multiple_of(chunks * chunk, chunk), capacity), :] = zeros
    for r in range(n_src):
        put(r, e, slot).start()

    @pl.when(e == local - 1)
    def _():
        @pl.when(e >= 1)
        def _():
            for r in range(n_src):
                put(r, e - 1, 1 - slot).wait()
        for r in range(n_src):
            put(r, e, slot).wait()


def experts(sizes, starts, totals, rows, gate_w, up_w, down_w):
    n_src, local, capacity, d_model = rows.shape
    width = gate_w.shape[2]
    chunk = capacity
    n_rows = n_src * capacity + 2 * capacity
    anywhere = pl.BlockSpec(memory_space=pl.ANY)
    return pl.pallas_call(
        functools.partial(expert_kernel, chunk=chunk),
        grid_spec=pltpu.PrefetchScalarGridSpec(
            num_scalar_prefetch=3,
            grid=(local,),
            in_specs=[anywhere] + [
                pl.BlockSpec((1, d_model, width), lambda e, *_: (e, 0, 0)),
                pl.BlockSpec((1, d_model, width), lambda e, *_: (e, 0, 0)),
                pl.BlockSpec((1, width, d_model), lambda e, *_: (e, 0, 0)),
            ],
            out_specs=anywhere,
            scratch_shapes=[
                pltpu.VMEM((2, n_rows, d_model), jnp.bfloat16),
                pltpu.VMEM((2, n_rows, d_model), jnp.bfloat16),
                pltpu.SemaphoreType.DMA((2, n_src)),
                pltpu.SemaphoreType.DMA((2, n_src)),
            ],
        ),
        out_shape=jax.ShapeDtypeStruct(rows.shape, jnp.bfloat16),
        compiler_params=params(),
        cost_estimate=pl.CostEstimate(flops=4 * local * n_src * capacity * d_model * width, bytes_accessed=6 * local * d_model * width, transcendentals=0),
        name="experts",
    )(sizes, starts, totals, rows, gate_w, up_w, down_w)


def neighbour(chips, swap=False):
    me, group = lax.axis_index('ep'), lax.axis_size('ep')
    side = lax.rem(me, 2)
    chip = lax.rem(me // 2 + chips + group // 2, group // 2)
    return {'ep': chip * 2 + (1 - side if swap else side)}


def greet():
    barrier = pltpu.get_barrier_semaphore()
    for device in (neighbour(1), neighbour(-1), neighbour(0, True)):
        pl.semaphore_signal(barrier, inc=1, device_id=device, device_id_type=pl.DeviceIdType.MESH)
    pl.semaphore_wait(barrier, 3)


def remote(src, dst, send_sem, recv_sem, device):
    return pltpu.make_async_remote_copy(src_ref=src, dst_ref=dst, send_sem=send_sem, recv_sem=recv_sem, device_id=device, device_id_type=pl.DeviceIdType.MESH)


def reduce_kernel(rank_ref, piece_ref, f_ref, out_ref, f_buf, spread, other_buf, swap_buf, send_buf, ring_buf, f_sems, swap_send, swap_recv, ring_send, ring_recv, out_sems, free_sem):
    n_src, n_tok, local = rank_ref.shape
    capacity = f_ref.shape[2]
    pieces = piece_ref.shape[2] // local
    chips = n_src // 2
    width = out_ref.shape[1] // 4
    n_units = 16

    def quarter(u):
        return 2 * lax.rem(u, 2) + u // 2

    def place(i):
        u = lax.rem(i, 4)
        odd = lax.rem(u, 2)
        target = jnp.where(i < 4, 1 + odd, jnp.where(i < 8, 2 - odd, jnp.where(i < 12, 3, 0)))
        return u, target

    def fetch(i, side, slot):
        u, target = place(i)
        cols = pl.ds(pl.multiple_of(quarter(u) * width, width), width)
        return pltpu.make_async_copy(f_ref.at[target + chips * (1 - side), :, :, cols], f_buf.at[slot, side], f_sems.at[slot, side])

    def swap_copy(i):
        s = lax.rem(i, 4)
        return remote(other_buf.at[s], swap_buf.at[s], swap_send.at[s], swap_recv.at[s], neighbour(0, True))

    def ring_copy(source, slot):
        return remote(send_buf.at[source], ring_buf.at[slot], ring_send.at[slot], ring_recv.at[slot], neighbour(1 - 2 * lax.rem(slot, 2)))

    def build(target, entry):
        @pl.loop(0, 2)
        def _(side):
            r = target + chips * (1 - side)
            rank = rank_ref[r]
            weights = piece_ref[r]
            slots = lax.broadcasted_iota(jnp.int32, (n_tok, capacity), 1)
            for e in range(local):
                hit = rank[:, e:e + 1] == slots
                for k in range(pieces):
                    column = k * local + e
                    spread[entry * 2 + side, k, :, e * capacity:(e + 1) * capacity] = jnp.where(hit, weights[:, column:column + 1], 0.0).astype(jnp.bfloat16)

    def product(entry, slot, side):
        data = jnp.concatenate([f_buf[slot, side, e] for e in range(local)], axis=0)
        total = jnp.dot(spread[entry * 2 + side, 0], data, preferred_element_type=jnp.float32)
        for k in range(1, pieces):
            total += jnp.dot(spread[entry * 2 + side, k], data, preferred_element_type=jnp.float32)
        return total

    for side in range(2):
        fetch(0, side, 0).start()
    greet()

    @pl.loop(0, n_units)
    def _(i):
        u, target = place(i)
        slot = lax.rem(i, 2)
        lane = lax.rem(i, 4)

        @pl.when(i + 1 < n_units)
        def _():
            for side in range(2):
                fetch(i + 1, side, 1 - slot).start()

        @pl.when(i == 0)
        def _():
            build(1, 0)

        @pl.when(i == 1)
        def _():
            build(2, 1)

        @pl.when(i == 8)
        def _():
            build(3, 0)

        @pl.when(i == 12)
        def _():
            build(0, 1)

        entry = 1 - lax.rem(target, 2)

        @pl.when(i >= 4)
        def _():
            swap_copy(i - 4).wait_send()
            pl.semaphore_wait(free_sem, 1)

        fetch(i, 0, slot).wait()
        other_buf[lane] = product(entry, slot, 0)
        swap_copy(i).start()
        fetch(i, 1, slot).wait()
        send_buf[i] = product(entry, slot, 1)
        swap_copy(i).wait_recv()
        send_buf[i] += swap_buf[lane]

        @pl.when(i < n_units - 4)
        def _():
            pl.semaphore_signal(free_sem, inc=1, device_id=neighbour(0, True), device_id_type=pl.DeviceIdType.MESH)

        @pl.when(i < 4)
        def _():
            ring_copy(i, u).start()

        @pl.when((i >= 8) & (i < 12))
        def _():
            ring_copy(i, u).wait_recv()
            send_buf[i] += ring_buf[u]
            ring_copy(i, u + 4).start()

    @pl.loop(0, 4)
    def _(u):
        ring_copy(0, u + 4).wait_recv()
        send_buf[u + 4] += ring_buf[u + 4]
        ring_copy(u + 4, u + 8).start()

    def put(u):
        cols = pl.ds(pl.multiple_of(quarter(u) * width, width), width)
        return pltpu.make_async_copy(send_buf.at[12 + u], out_ref.at[:, cols], out_sems.at[u])

    @pl.loop(0, 4)
    def _(u):
        ring_copy(0, u + 8).wait_recv()
        send_buf[12 + u] += ring_buf[u + 8]
        put(u).start()

    @pl.loop(0, 4)
    def _(u):
        put(u).wait()
        swap_copy(n_units - 4 + u).wait_send()
        ring_copy(u, u).wait_send()
        ring_copy(8 + u, u + 4).wait_send()
        ring_copy(4 + u, u + 8).wait_send()


def reduce_results(rank_t, pieces, results):
    n_src, local, capacity, d_model = results.shape
    n_tok = rank_t.shape[1]
    width = d_model // 4
    n_pieces = pieces.shape[2] // local
    tile = (n_tok, width)
    vmem = pl.BlockSpec(memory_space=pltpu.VMEM)
    return pl.pallas_call(
        reduce_kernel,
        in_specs=[vmem, vmem, pl.BlockSpec(memory_space=pl.ANY)],
        out_specs=pl.BlockSpec(memory_space=pl.ANY),
        out_shape=jax.ShapeDtypeStruct((n_tok, d_model), jnp.float32),
        scratch_shapes=[
            pltpu.VMEM((2, 2, local, capacity, width), jnp.bfloat16),
            pltpu.VMEM((4, n_pieces, n_tok, local * capacity), jnp.bfloat16),
            pltpu.VMEM((4,) + tile, jnp.float32),
            pltpu.VMEM((4,) + tile, jnp.float32),
            pltpu.VMEM((16,) + tile, jnp.float32),
            pltpu.VMEM((12,) + tile, jnp.float32),
            pltpu.SemaphoreType.DMA((2, 2)),
            pltpu.SemaphoreType.DMA((4,)),
            pltpu.SemaphoreType.DMA((4,)),
            pltpu.SemaphoreType.DMA((12,)),
            pltpu.SemaphoreType.DMA((12,)),
            pltpu.SemaphoreType.DMA((4,)),
            pltpu.SemaphoreType.REGULAR,
        ],
        compiler_params=pltpu.CompilerParams(vmem_limit_bytes=MAX_VMEM, collective_id=2, has_side_effects=True),
        cost_estimate=pl.CostEstimate(flops=6 * n_src * local * capacity * n_tok * d_model, bytes_accessed=4 * n_src * local * capacity * d_model, transcendentals=0),
        name="reduce_results",
    )(rank_t, pieces, results)


def bf16_pieces(values):
    first = lax.reduce_precision(values, 8, 7)
    second = lax.reduce_precision(values - first, 8, 7)
    third = values - first - second
    return first, second, third


def local_layer(x_loc, q_shard, k_shard, v_shard, o_shard, w_router, gate_loc, up_loc, down_loc, sgate_shard, sup_shard, sdown_shard, ids_loc, group):
    n_seq, seq_len, d_model = x_loc.shape
    head = q_shard.shape[2]
    n_tok = n_seq * seq_len
    top_k = ids_loc.shape[-1]
    local = gate_loc.shape[0]
    n_experts = local * group
    capacity = CAP_FACTOR * n_tok * top_k // n_experts
    me = lax.axis_index('ep')
    chips = [me // 2 + step for step in (0, -1, 1, 2)]
    order = jnp.stack([(c % (group // 2)) * 2 + side for side in (me % 2, 1 - me % 2) for c in chips]).astype(jnp.int32)

    def gathered(shard):
        return lax.all_gather(shard.reshape(shard.shape[0], -1), 'ep', axis=0, tiled=True)

    def project(rows, weight):
        return jnp.dot(rows, weight, preferred_element_type=jnp.float32).astype(jnp.bfloat16)

    ids_all = lax.all_gather(ids_loc.reshape(n_tok, top_k).T, 'ep', axis=0)[order]
    mine = lax.axis_index('ep') * local + jnp.arange(local)
    chosen = ids_all[:, None, :, :] == mine[None, :, None, None]
    member = jnp.any(chosen, axis=2)
    before = (jnp.arange(n_tok)[:, None] < jnp.arange(n_tok)[None, :]).astype(jnp.bfloat16)
    rank = jnp.einsum('set,tq->seq', member.astype(jnp.bfloat16), before, preferred_element_type=jnp.float32).astype(jnp.int32)
    rank = jnp.where(member, rank, -1)
    rank_t = rank.transpose(0, 2, 1)
    sizes = (jnp.sum(member.astype(jnp.int32), axis=2) + ALIGN - 1) // ALIGN * ALIGN
    ends = jnp.cumsum(sizes, axis=0)
    starts, totals = ends - sizes, ends[-1]

    x_flat = x_loc.reshape(n_tok, d_model)
    normed = rms_norm(x_flat).astype(jnp.bfloat16)
    keys_all = project(normed, gathered(k_shard))
    vals_all = project(normed, gathered(v_shard))
    queries = project(normed, gathered(q_shard))
    attended = [attention(queries[i * seq_len:(i + 1) * seq_len], keys_all[i * seq_len:(i + 1) * seq_len], vals_all[i * seq_len:(i + 1) * seq_len], head) for i in range(n_seq)]
    attended = attended[0] if n_seq == 1 else jnp.concatenate(attended, axis=0)
    attn_out = project(attended, gathered(o_shard))
    residual = (x_flat.astype(jnp.float32) + attn_out.astype(jnp.float32)).astype(jnp.bfloat16)

    hidden = rms_norm(residual)
    moe_in = hidden.astype(jnp.bfloat16)
    tokens = lax.all_gather(moe_in, 'ep', axis=0)
    logits = jnp.dot(hidden, w_router, precision=lax.Precision.HIGHEST, preferred_element_type=jnp.float32)
    tok_ids = ids_loc.reshape(n_tok, top_k)
    picked = tok_ids[:, :, None] == jnp.arange(n_experts)[None, None, :]
    chosen_logits = jnp.sum(jnp.where(picked, logits[:, None, :], 0.0), axis=2)
    gate_probs = jax.nn.softmax(chosen_logits, axis=-1)
    gates_all = lax.all_gather(gate_probs.T, 'ep', axis=0)[order]
    weight = jnp.sum(jnp.where(chosen, gates_all[:, None, :, :], 0.0), axis=2)
    pieces = jnp.concatenate(bf16_pieces(weight), axis=1).transpose(0, 2, 1)

    rows = dispatch(order, rank, tokens, capacity)
    results = experts(sizes, starts, totals, rows, gate_loc, up_loc, down_loc)

    gate_act = jnp.dot(moe_in, gathered(sgate_shard), preferred_element_type=jnp.float32)
    up_act = jnp.dot(moe_in, gathered(sup_shard), preferred_element_type=jnp.float32)
    middle = (jax.nn.silu(gate_act) * up_act).astype(jnp.bfloat16)
    shared = project(middle, gathered(sdown_shard))
    routed = reduce_results(rank_t, pieces, results)
    y_out = (residual.astype(jnp.float32) + routed + shared.astype(jnp.float32)).astype(jnp.bfloat16)
    return y_out.reshape(n_seq, seq_len, d_model)


def solution(mesh):
    tok_spec = P(('dp', 'ep'), None, None)
    row_spec = P('ep', None)
    cube_spec = P('ep', None, None)
    in_specs = (tok_spec, cube_spec, cube_spec, cube_spec, row_spec, P(None, None), cube_spec, cube_spec, cube_spec, row_spec, row_spec, row_spec, tok_spec)
    return jax.shard_map(functools.partial(local_layer, group=mesh.shape['ep']), mesh=mesh, in_specs=in_specs, out_specs=tok_spec, check_vma=False)
```

time: 693 us -> 619 us (0.89); the launches traced: 692 us -> 609 us
  waiting for transfers between devices: 347 us -> 200 us
  Pallas kernels: 226 us -> 288 us
    reduce_scatter x1 -> x0, waiting for transfers between devices: 160 us -> none  [local_layer(): lax.psum_scatter(partial.reshape(group * n_tok, d_model), 'ep', scatter_d...]
    pallas_call x2, Pallas kernels: 182 us -> 244 us  [the longest x1 157 us: reduce_results(): pl.pallas_call(reduce_kernel, in_specs=[vmem, vmem, pl.BlockSpec(memory_s...]
    all_gather x1, waiting for transfers between devices: 41 us -> 53 us  [local_layer(): tokens = lax.all_gather(moe_in, 'ep', axis=0)]
  transfers between devices with their start and end apart: 9 -> 8, of which waited for: 6 -> 5; matrix products, arithmetic and copies ran while one was open for 8% -> 11% of each run, Pallas kernels for 33% -> 47%
where the time goes in v2:
time: 619 us; the launch traced here: 609 us
  Pallas kernels  288 us (47%)
  waiting for transfers between devices  200 us (32%)
  matrix products  61.8 us (10%)
  blocking collectives  26.3 us (4%)
  local copies, waits for them, and re-layouts  14.5 us (2%)
  between operations  14.3 us (2%)
    pallas_call x1, Pallas kernels, reduce_results(): pl.pallas_call(reduce_kernel, in_specs=[vmem, vmem, pl.BlockSpec(memory_s...  157 us
    all_gather x7, waiting for transfers between devices, gathered(): lax.all_gather(shard.reshape(shard.shape[0], -1), 'ep', axis=0, tiled=True)  144 us
    pallas_call x1, Pallas kernels, experts(): pl.pallas_call(functools.partial(expert_kernel, chunk=chunk), grid_spec=p...  86.9 us
    all_gather x1, waiting for transfers between devices, local_layer(): tokens = lax.all_gather(moe_in, 'ep', axis=0)  53 us
    dot_general x5, matrix products, project(): jnp.dot(rows, weight, preferred_element_type=jnp.float32)  49.3 us
    pallas_call x1, Pallas kernels, dispatch(): pl.pallas_call(functools.partial(dispatch_kernel, capacity=capacity), gri...  26 us
    pallas_call x1, Pallas kernels, attention(): pl.pallas_call(functools.partial(attention_kernel, parts=2), grid=(width...  18.2 us
    all_gather x1, blocking collectives, local_layer(): lax.all_gather(ids_loc.reshape(n_tok, top_k).T, 'ep', axis=0)[order]  13.2 us
  transfers between devices with their start and end apart: 8, of which 5 were waited for; matrix products, arithmetic and copies ran while one was open for 11% of the time, Pallas kernels for 47%

profile of v2, /device:TPU:81, one launch (start us, length us, event | category | flops | bytes accessed | tf_op | source)
XLA Modules:
  0.0 609.5 jit_solution(1830729422178761502)
XLA Ops:
  6.6 2.6 copy.41
  9.3 2.6 copy.42
  15.2 45.1 %all-gather.16.cloned.1.call-done = bf16[2048,2048]{1,0:T(8,128)(2,1)} async-done(((bf16[256,2048]{1,0:T(8,128)(2,1)}), bf16[2048,2048]{1,0:T(8,128)(2,1)}) %all-gather.16.cloned.1.call-update) | async-done | bytes 8388624 | tf_op jit(solution)/shard_map/all_gather | solution.py:381
  60.3 9.2 %convolution_convert_fusion.2.v_ref = bf16[512,2048]{1,0:T(8,128)(2,1)} fusion(bf16[2048,2048]{1,0:T(8,128)(2,1)} %all-gather.16.cloned.1.call-done, bf16[1,512,2048]{2,1,0:T(8,128)(2,1)S(1)} %copy-done.1, f32[512]{0:T(512)S(1)} %add_rsqrt_fusion.1), kind=kOutput, calls=%fused_computation.18 | convolution fusion | flops 4299161600 | bytes 12584960 | tf_op jit(solution)/shard_map/dot_general | solution.py:384
  69.5 39.0 %all-gather.14.cloned.1.call-done = bf16[2048,2048]{1,0:T(8,128)(2,1)} async-done(((bf16[256,2048]{1,0:T(8,128)(2,1)}), bf16[2048,2048]{1,0:T(8,128)(2,1)}) %all-gather.14.cloned.1.call-update) | async-done | bytes 8388624 | tf_op jit(solution)/shard_map/all_gather | solution.py:381
  108.6 9.2 %convolution_convert_fusion.3.k_ref = bf16[512,2048]{1,0:T(8,128)(2,1)} fusion(bf16[2048,2048]{1,0:T(8,128)(2,1)} %all-gather.14.cloned.1.call-done, bf16[1,512,2048]{2,1,0:T(8,128)(2,1)S(1)} %copy-done.1, f32[512]{0:T(512)S(1)} %add_rsqrt_fusion.1), kind=kOutput, calls=%fused_computation.19 | convolution fusion | flops 4299161600 | bytes 12584960 | tf_op jit(solution)/shard_map/dot_general | solution.py:384
  117.8 39.1 %all-gather.12.cloned.1.call-done = bf16[2048,2048]{1,0:T(8,128)(2,1)} async-done(((bf16[256,2048]{1,0:T(8,128)(2,1)}), bf16[2048,2048]{1,0:T(8,128)(2,1)}) %all-gather.12.cloned.1.call-update) | async-done | bytes 8388624 | tf_op jit(solution)/shard_map/all_gather | solution.py:381
  156.9 9.2 %convolution_convert_fusion.4.q_ref = bf16[512,2048]{1,0:T(8,128)(2,1)} fusion(bf16[2048,2048]{1,0:T(8,128)(2,1)} %all-gather.12.cloned.1.call-done, bf16[1,512,2048]{2,1,0:T(8,128)(2,1)S(1)} %copy-done.1, f32[512]{0:T(512)S(1)} %add_rsqrt_fusion.1), kind=kOutput, calls=%fused_computation.20 | convolution fusion | flops 4299161600 | bytes 12584960 | tf_op jit(solution)/shard_map/dot_general | solution.py:384
  166.1 18.2 %attention.1 = bf16[512,2048]{1,0:T(8,128)(2,1)} custom-call(bf16[512,2048]{1,0:T(8,128)(2,1)} %convolution_convert_fusion.4.q_ref, bf16[512,2048]{1,0:T(8,128)(2,1)} %convolution_convert_fusion.3.k_ref, bf16[512,2048]{1,0:T(8,128)(2,1)} %convolution_convert_fusion.2.v_ref), custom_call_target="tpu_custom_call" | custom-call | flops 4294967296 | bytes 8388608 | tf_op jit(solution)/shard_map/attention/pallas_call | solution.py:42
  184.3 20.7 %all-gather.18.cloned.1.call-done = bf16[2048,2048]{1,0:T(8,128)(2,1)} async-done(((bf16[256,2048]{1,0:T(8,128)(2,1)}), bf16[2048,2048]{1,0:T(8,128)(2,1)}) %all-gather.18.cloned.1.call-update) | async-done | bytes 8388624 | tf_op jit(solution)/shard_map/all_gather | solution.py:381
  205.0 9.3 %fusion.2 = (f32[512]{0:T(512)S(1)}, bf16[512,2048]{1,0:T(8,128)(2,1)S(1)}) fusion(bf16[512,2048]{1,0:T(8,128)(2,1)} %attention.1, bf16[2048,2048]{1,0:T(8,128)(2,1)} %all-gather.18.cloned.1.call-done, bf16[1,512,2048]{2,1,0:T(8,128)(2,1)} %param.13), kind=kOutput, calls=%fused_computation.10 | convolution fusion | flops 4303355392 | bytes 14682112 | tf_op jit(solution)/shard_map/dot_general | solution.py:384
  214.3 1.9 fusion
  218.2 13.2 %all-gather = s32[64,512]{1,0:T(8,128)S(1)} all-gather(s32[8,512]{1,0:T(8,128)S(1)} %bitcast.75), channel_id=2, replica_groups=mesh['dp'=4,'ep'=8] {'ep'}, dimensions={0}, use_global_device_ids=true | all-gather | bytes 147456 | tf_op jit(solution)/shard_map/all_gather | solution.py:386
  234.6 2.2 convert_select_fusion
  236.8 2.8 copy.33.rank_ref
  240.2 4.4 fusion.1
  244.9 13.1 %all-gather.1 = f32[64,512]{1,0:T(8,128)S(1)} all-gather(f32[8,512]{1,0:T(8,128)S(1)} %divide_bitcast_fusion), channel_id=3, replica_groups=mesh['dp'=4,'ep'=8] {'ep'}, dimensions={0}, use_global_device_ids=true | all-gather | bytes 147456 | tf_op jit(solution)/shard_map/all_gather | solution.py:416
  259.0 2.0 copy.32
  261.0 5.9 fusion.26
  266.9 53.0 %all-gather.26.cloned.1.call-done = bf16[4096,2048]{1,0:T(8,128)(2,1)} async-done(((bf16[512,2048]{1,0:T(8,128)(2,1)}), bf16[4096,2048]{1,0:T(8,128)(2,1)}) %all-gather.26.cloned.1.call-update) | async-done | bytes 16777232 | tf_op jit(solution)/shard_map/all_gather | solution.py:410
  319.9 26.0 %dispatch.1.x_ref = bf16[8,8,128,2048]{3,2,1,0:T(8,128)(2,1)} custom-call(s32[8]{0:T(128)} %stack.62.order_ref, s32[8,8,512]{2,1,0:T(8,128)} %copy.33.rank_ref, bf16[8,512,2048]{2,1,0:T(8,128)(2,1)} %bitcast.77), custom_call_target="tpu_custom_call" | custom-call | flops 17179869184 | bytes 67108864 | tf_op jit(solution)/shard_map/dispatch/pallas_call | solution.py:70
  345.9 86.9 %experts.1.f_ref = bf16[8,8,128,2048]{3,2,1,0:T(8,128)(2,1)} custom-call(s32[8,8]{1,0:T(8,128)} %copy-done.6, s32[8,8]{1,0:T(8,128)} %fusion.19.start_ref, s32[8]{0:T(128)} %slice_bitcast_fusion.total_ref, bf16[8,8,128,2048]{3,2,1,0:T(8,128)(2,1)} %dispatch.1.x_ref, bf16[8,2048,1024]{2,1,0:T(8,128)(2,1)} %gate_ref.1, bf16[8,2048,1024]{2,1,0:T(8,128)(2,1)} %up_ref.1, ...), custom_call_target="tpu_custom_call" | custom-call | flops 68719476736 | bytes 100663296 | tf_op jit(solution)/shard_map/experts/pallas_call | solution.py:151
  432.8 157.0 %reduce_results.1 = f32[512,2048]{1,0:T(8,128)} custom-call(s32[8,512,8]{2,1,0:T(8,128)} %bitcast.69, f32[8,512,24]{2,1,0:T(8,128)} %bitcast.68, bf16[8,8,128,2048]{3,2,1,0:T(8,128)(2,1)} %experts.1.f_ref), custom_call_target="tpu_custom_call" | custom-call | flops 51539607552 | bytes 67108864 | tf_op jit(solution)/shard_map/reduce_results/pallas_call | solution.py:335
  589.8 12.4 %fusion.8 = bf16[1,512,2048]{2,1,0:T(8,128)(2,1)} fusion(bf16[1024,2048]{1,0:T(8,128)(2,1)} %all-gather.24.cloned.1.call-done, f32[512,2048]{1,0:T(8,128)} %reduce_results.1, bf16[512,2048]{1,0:T(8,128)(2,1)} %copy-done, f32[512,1024]{1,0:T(8,128)} %fusion.26, bf16[2048,1024]{1,0:T(8,128)(2,1)} %all-gather.22.cloned.1.call-done, f32[512]{0:T(512)} %copy-done.5), kind=kOutput, calls=%fused_computation.21 | convolution fusion | flops 4307550208 | bytes 18876416 | tf_op jit(solution)/shard_map/dot_general | solution.py:384
  (58 shorter events, 10.2 us)
Async XLA Ops:
  6.5 5.5 copy-start.2
  6.5 53.7 %all-gather.16.cloned.1.call-start = ((), (), s32[]{:S(2)}) async-start(), calls=%async_computation.2 | async-start | bytes 9437184 | tf_op jit(solution)/shard_map/all_gather | solution.py:381
  9.2 5.5 copy-start.1
  9.2 99.4 %all-gather.14.cloned.1.call-start = ((), (), s32[]{:S(2)}) async-start(), calls=%async_computation.1 | async-start | bytes 9437184 | tf_op jit(solution)/shard_map/all_gather | solution.py:381
  11.9 144.9 %all-gather.12.cloned.1.call-start = ((), (), s32[]{:S(2)}) async-start(), calls=%async_computation | async-start | bytes 9437184 | tf_op jit(solution)/shard_map/all_gather | solution.py:381
  13.3 191.7 %all-gather.18.cloned.1.call-start = ((), (), s32[]{:S(2)}) async-start(), calls=%async_computation.3 | async-start | bytes 9437184 | tf_op jit(solution)/shard_map/all_gather | solution.py:381
  14.0 247.0 %all-gather.20.cloned.1.call-start = ((), (), s32[]{:S(2)}) async-start(), calls=%async_computation.4 | async-start | bytes 4718592 | tf_op jit(solution)/shard_map/all_gather | solution.py:381
  14.6 305.3 %all-gather.26.cloned.1.call-start = ((), (), s32[]{:S(2)}) async-start(), calls=%async_computation.7 | async-start | bytes 18874368 | tf_op jit(solution)/shard_map/all_gather | solution.py:410
  214.3 46.7 %copy-start = (bf16[512,2048]{1,0:T(8,128)(2,1)}, bf16[512,2048]{1,0:T(8,128)(2,1)S(1)}, u32[]{:S(2)}) copy-start(bf16[512,2048]{1,0:T(8,128)(2,1)S(1)} %get-tuple-element.9) | copy-start | bytes 6291460
  214.3 3.8 copy-start.4
  214.3 52.5 %copy-start.5 = (f32[512]{0:T(512)}, f32[512]{0:T(512)S(1)}, u32[]{:S(2)}) copy-start(f32[512]{0:T(512)S(1)} %add_rsqrt_fusion) | copy-start | bytes 6148
  216.3 373.5 %all-gather.22.cloned.1.call-start = ((), (), s32[]{:S(2)}) async-start(), calls=%async_computation.5 | async-start | bytes 4718592 | tf_op jit(solution)/shard_map/all_gather | solution.py:381
  217.1 23.1 %copy-start.3 = (f32[2048,64]{0,1:T(8,128)S(1)}, f32[2048,64]{0,1:T(8,128)}, u32[]{:S(2)}) copy-start(f32[2048,64]{0,1:T(8,128)} %param.18) | copy-start | bytes 1572868
  217.1 372.7 %all-gather.24.cloned.1.call-start = ((), (), s32[]{:S(2)}) async-start(), calls=%async_computation.6 | async-start | bytes 4718592 | tf_op jit(solution)/shard_map/all_gather | solution.py:381
  233.4 11.3 %copy-start.6 = (s32[8,8]{1,0:T(8,128)}, s32[8,8]{1,0:T(8,128)S(1)}, u32[]{:S(2)}) copy-start(s32[8,8]{1,0:T(8,128)S(1)} %fusion.15.size_ref) | copy-start | bytes 772
Sparse Core Ops, SparseCore 0:
  9.3 50.9 all-gather.15
  61.9 46.6 all-gather.13
  110.2 46.6 all-gather.11
  158.3 46.6 all-gather.17
  206.5 29.4 all-gather.19
  237.5 82.4 all-gather.25
  321.5 29.1 all-gather.21
  352.4 28.6 all-gather.23

commit v3 on v2

--- a/solution.py
+++ b/solution.py
@@ -22,64 +22,315 @@
     return pltpu.CompilerParams(vmem_limit_bytes=VMEM_BYTES, **kw)
 
 
-def attention_kernel(q_ref, k_ref, v_ref, o_ref, *, parts):
-    seq, head = q_ref.shape
-    step = seq // parts
-    for part in range(parts):
-        lo, hi = part * step, (part + 1) * step
-        scores = lax.dot_general(q_ref[lo:hi, :], k_ref[:hi, :], (((1,), (1,)), ((), ())), preferred_element_type=jnp.float32) * (head ** -0.5)
-        rows = lo + lax.broadcasted_iota(jnp.int32, scores.shape, 0)
-        cols = lax.broadcasted_iota(jnp.int32, scores.shape, 1)
-        scores = jnp.where(rows >= cols, scores, -1e30)
-        weights = jnp.exp(scores - jnp.max(scores, axis=-1, keepdims=True))
-        probs = (weights / jnp.sum(weights, axis=-1, keepdims=True)).astype(jnp.bfloat16)
-        o_ref[lo:hi, :] = jnp.dot(probs, v_ref[:hi, :], preferred_element_type=jnp.float32).astype(jnp.bfloat16)
-
-
-def attention(queries, keys, vals, head):
-    seq, width = queries.shape
-    spec = pl.BlockSpec((seq, head), lambda i: (0, i))
+def neighbour(chips, swap=False):
+    me, group = lax.axis_index('ep'), lax.axis_size('ep')
+    side = lax.rem(me, 2)
+    chip = lax.rem(me // 2 + chips + group // 2, group // 2)
+    return {'ep': chip * 2 + (1 - side if swap else side)}
+
+
+def greet(*devices):
+    barrier = pltpu.get_barrier_semaphore()
+    for device in devices:
+        pl.semaphore_signal(barrier, inc=1, device_id=device, device_id_type=pl.DeviceIdType.MESH)
+    pl.semaphore_wait(barrier, len(devices))
+
+
+def remote(src, dst, send_sem, recv_sem, device):
+    return pltpu.make_async_remote_copy(src_ref=src, dst_ref=dst, send_sem=send_sem, recv_sem=recv_sem, device_id=device, device_id_type=pl.DeviceIdType.MESH)
+
+
+class Gather:
+    def __init__(self, buf, send, recv, split=True):
+        other = neighbour(0, True)
+        half = buf.shape[1] // 2
+        lo, hi = pl.ds(0, half), pl.ds(half, half)
+
+        def copy(k, src, dst, device):
+            return remote(src, dst, send.at[k], recv.at[k], device)
+
+        self.own = [copy(0, buf.at[0], buf.at[1], neighbour(1)), copy(1, buf.at[0], buf.at[2], neighbour(-1))]
+        self.mate = [copy(2, buf.at[0], buf.at[4], other)]
+        self.near_mate = [copy(3, buf.at[1], buf.at[5], other), copy(4, buf.at[2], buf.at[6], other)]
+        if split:
+            self.far = [copy(5, buf.at[1, lo], buf.at[3, lo], neighbour(1)), copy(6, buf.at[2, hi], buf.at[3, hi], neighbour(-1))]
+            self.far_mate = [copy(7, buf.at[3, lo], buf.at[7, lo], other), copy(8, buf.at[3, hi], buf.at[7, hi], other)]
+        else:
+            self.far = [copy(5, buf.at[0], buf.at[3], neighbour(2))]
+            self.far_mate = [copy(7, buf.at[3], buf.at[7], other)]
+        self.split = split
+
+    def begin(self):
+        for copy in self.own + self.mate + ([] if self.split else self.far):
+            copy.start()
+
+    def forward(self):
+        for k in range(2):
+            self.own[k].wait_recv()
+            if self.split:
+                self.far[k].start()
+            self.near_mate[k].start()
+
+    def forward_far(self):
+        for copy, mate in zip(self.far, self.far_mate):
+            copy.wait_recv()
+            mate.start()
+
+    def arrive(self, copies):
+        for copy in copies:
+            copy.wait_recv()
+
+    def finish(self):
+        for copy in self.own + self.mate + self.near_mate + self.far + self.far_mate:
+            copy.wait_send()
+
+
+def owner(r):
+    step = (0, -1, 1, 2)[r % 4]
+    return neighbour(step, r >= 4)['ep']
+
+
+def attention_layer_kernel(x_ref, ids_ref, k_hbm, v_hbm, q_hbm, o_hbm, h_ref, rank_ref, ids_out, w_buf, n_buf, qkv, ids_buf, load_sems, send, recv, ids_send, ids_recv):
+    n_tok, d_model = x_ref.shape
+    group, local = rank_ref.shape[:2]
+    size = d_model // group
+    head = 128
+    width = 512
+    keys, vals, queries, outs = range(4)
+    gathers = [Gather(w_buf.at[w], send.at[w], recv.at[w]) for w in range(4)]
+    ids_gather = Gather(ids_buf, ids_send, ids_recv, split=False)
+    loads = [pltpu.make_async_copy(ref, w_buf.at[w, 0], load_sems.at[w]) for w, ref in enumerate((k_hbm, v_hbm, q_hbm, o_hbm))]
+    ids_load = pltpu.make_async_copy(ids_ref, ids_buf.at[0], load_sems.at[4])
+    ids_load.start()
+    for load in loads:
+        load.start()
+    greet(neighbour(1), neighbour(-1), neighbour(2), neighbour(0, True))
+    ids_load.wait()
+    ids_gather.begin()
+    for w in (keys, vals):
+        loads[w].wait()
+        gathers[w].begin()
+
+    @pl.loop(0, n_tok // 128)
+    def _(i):
+        rows = pl.ds(pl.multiple_of(i * 128, 128), 128)
+        normed = rms_norm(x_ref[rows, :]).astype(jnp.bfloat16)
+        qkv[0, rows, :] = normed
+        for r in range(group):
+            n_buf[rows, r * size:(r + 1) * size] = qkv[0, rows, pl.ds(pl.multiple_of(owner(r) * size, size), size)]
+
+    ids_gather.arrive(ids_gather.own + ids_gather.mate)
+    for copy in ids_gather.near_mate:
+        copy.start()
+    ids_gather.forward_far()
+    ids_gather.arrive(ids_gather.near_mate + ids_gather.far_mate)
+    first = lax.axis_index('ep') * local
+    before = (lax.broadcasted_iota(jnp.int32, (n_tok, n_tok), 0) < lax.broadcasted_iota(jnp.int32, (n_tok, n_tok), 1)).astype(jnp.float32).astype(jnp.bfloat16)
+    for r in range(group):
+        member = jnp.concatenate([jnp.max((ids_buf[r] == first + e).astype(jnp.float32), axis=0, keepdims=True) for e in range(local)], axis=0)
+        rank = jnp.dot(member.astype(jnp.bfloat16), before, preferred_element_type=jnp.float32)
+        rank_ref[r] = jnp.where(member > 0.5, rank, -1.0).astype(jnp.int32)
+
+    def project(w, store):
+        @pl.loop(0, d_model // width)
+        def _(c):
+            cols = pl.ds(pl.multiple_of(c * width, width), width)
+            weight = jnp.concatenate([w_buf[w, r, :, cols] for r in range(group)], axis=0)
+            store(cols, jnp.dot(n_buf[...], weight, preferred_element_type=jnp.float32).astype(jnp.bfloat16))
+
+    def keep(w):
+        def store(cols, values):
+            qkv[w, :, cols] = values
+        return store
+
+    def complete(w):
+        gathers[w].forward_far()
+        gathers[w].arrive(gathers[w].mate + gathers[w].near_mate + gathers[w].far_mate)
+
+    def attend(lo, hi):
+        for r in range(lo, hi):
+            start = owner(r) * size
+
+            @pl.loop(0, size // head)
+            def _(k):
+                cols = pl.ds(pl.multiple_of(start + k * head, head), head)
+                parts = 2
+                step = n_tok // parts
+                for part in range(parts):
+                    top, end = part * step, (part + 1) * step
+                    scores = lax.dot_general(qkv[queries, top:end, cols], qkv[keys, :end, cols], (((1,), (1,)), ((), ())), preferred_element_type=jnp.float32) * (head ** -0.5)
+                    row = top + lax.broadcasted_iota(jnp.int32, scores.shape, 0)
+                    col = lax.broadcasted_iota(jnp.int32, scores.shape, 1)
+                    scores = jnp.where(row >= col, scores, -1e30)
+                    weights = jnp.exp(scores - jnp.max(scores, axis=-1, keepdims=True))
+                    probs = (weights / jnp.sum(weights, axis=-1, keepdims=True)).astype(jnp.bfloat16)
+                    n_buf[top:end, pl.ds(pl.multiple_of(r * size + k * head, head), head)] = jnp.dot(probs, qkv[vals, :end, cols], preferred_element_type=jnp.float32).astype(jnp.bfloat16)
+
+    gathers[keys].forward()
+    loads[queries].wait()
+    gathers[queries].begin()
+    gathers[vals].forward()
+    complete(keys)
+    project(keys, keep(keys))
+    gathers[queries].forward()
+    loads[outs].wait()
+    gathers[outs].begin()
+    complete(vals)
+    project(vals, keep(vals))
+    complete(queries)
+    project(queries, keep(queries))
+    attend(0, group // 2)
+    gathers[outs].forward()
+    attend(group // 2, group)
+    complete(outs)
+
+    def residual(cols, values):
+        h_ref[:, cols] = (x_ref[:, cols].astype(jnp.float32) + values.astype(jnp.float32)).astype(jnp.bfloat16)
+
+    project(outs, residual)
+    for r in range(group):
+        ids_out[r] = ids_buf[r]
+    for gather in gathers + [ids_gather]:
+        gather.finish()
+
+
+def attention_layer(x, ids_t, k_shard, v_shard, q_shard, o_shard, group, local):
+    n_tok, d_model = x.shape
+    top_k = ids_t.shape[0]
+    vmem = pl.BlockSpec(memory_space=pltpu.VMEM)
+    anywhere = pl.BlockSpec(memory_space=pl.ANY)
     return pl.pallas_call(
-        functools.partial(attention_kernel, parts=2),
-        grid=(width // head,),
-        in_specs=[spec] * 3,
-        out_specs=spec,
-        out_shape=jax.ShapeDtypeStruct((seq, width), jnp.bfloat16),
-        compiler_params=params(),
-        cost_estimate=pl.CostEstimate(flops=8 * seq * seq * width, bytes_accessed=8 * seq * width, transcendentals=0),
-        name="attention",
-    )(queries, keys, vals)
-
-
-def dispatch_kernel(order_ref, rank_ref, u_ref, x_ref, *, capacity):
-    local, n_tok = rank_ref.shape[1:]
-    slots = lax.broadcasted_iota(jnp.int32, (capacity, n_tok), 0)
-    picks = [(rank_ref[0, e:e + 1, :] == slots).astype(jnp.float32).astype(jnp.bfloat16) for e in range(local)]
-    pick = jnp.concatenate(picks, axis=0)
+        attention_layer_kernel,
+        in_specs=[vmem] + [anywhere] * 5,
+        out_specs=[vmem] * 3,
+        out_shape=[jax.ShapeDtypeStruct(x.shape, jnp.bfloat16), jax.ShapeDtypeStruct((group, local, n_tok), jnp.int32), jax.ShapeDtypeStruct((group, top_k, n_tok), jnp.int32)],
+        scratch_shapes=[
+            pltpu.VMEM((4, group) + k_shard.shape, jnp.bfloat16),
+            pltpu.VMEM(x.shape, jnp.bfloat16),
+            pltpu.VMEM((3,) + x.shape, jnp.bfloat16),
+            pltpu.VMEM((group, top_k, n_tok), jnp.int32),
+            pltpu.SemaphoreType.DMA((5,)),
+            pltpu.SemaphoreType.DMA((4, 9)),
+            pltpu.SemaphoreType.DMA((4, 9)),
+            pltpu.SemaphoreType.DMA((9,)),
+            pltpu.SemaphoreType.DMA((9,)),
+        ],
+        compiler_params=pltpu.CompilerParams(vmem_limit_bytes=MAX_VMEM, collective_id=0, has_side_effects=True),
+        cost_estimate=pl.CostEstimate(flops=9 * n_tok * d_model * d_model, bytes_accessed=8 * d_model * d_model // group, transcendentals=0),
+        name="attention_layer",
+    )(x, ids_t, k_shard, v_shard, q_shard, o_shard)
+
+
+def dispatch_kernel(h_ref, wr_ref, ids_ref, rank_ref, x_hbm, gates_ref, u_buf, pick, stage, g_buf, out_sems, send, recv, g_send, g_recv):
+    n_tok, d_model = h_ref.shape
+    group, local = rank_ref.shape[:2]
+    capacity = x_hbm.shape[2]
+    n_experts = wr_ref.shape[0]
+    top_k = ids_ref.shape[0]
+    width = stage.shape[3]
+    n_cols = d_model // width
+    tokens = Gather(u_buf, send, recv)
+    gates = Gather(g_buf, g_send, g_recv, split=False)
+
+    @pl.loop(0, n_tok // 128)
+    def _(i):
+        rows = pl.ds(pl.multiple_of(i * 128, 128), 128)
+        u_buf[0, rows, :] = rms_norm(h_ref[rows, :]).astype(jnp.bfloat16)
+
+    greet(neighbour(1), neighbour(-1), neighbour(2), neighbour(0, True))
+    tokens.begin()
+
+    for i in range(n_tok // 128):
+        rows = slice(i * 128, (i + 1) * 128)
+        logits = lax.dot_general(wr_ref[...], rms_norm(h_ref[rows, :]), (((1,), (1,)), ((), ())), precision=lax.Precision.HIGHEST, preferred_element_type=jnp.float32)
+        experts_iota = lax.broadcasted_iota(jnp.int32, (n_experts, 128), 0)
+        chosen = jnp.concatenate([jnp.sum(jnp.where(experts_iota == ids_ref[j:j + 1, rows], logits, 0.0), axis=0, keepdims=True) for j in range(top_k)], axis=0)
+        weights = jnp.exp(chosen - jnp.max(chosen, axis=0, keepdims=True))
+        g_buf[0, :, rows] = weights / jnp.sum(weights, axis=0, keepdims=True)
+    gates.begin()
+
+    def put(r, c, slot):
+        cols = pl.ds(pl.multiple_of(c * width, width), width)
+        return pltpu.make_async_copy(stage.at[slot], x_hbm.at[r, :, :, cols], out_sems.at[slot])
+
+    def dispatch(r, before):
+        slots = lax.broadcasted_iota(jnp.int32, (capacity, n_tok), 0)
+        for e in range(local):
+            pick[e * capacity:(e + 1) * capacity, :] = (rank_ref[r, e:e + 1, :] == slots).astype(jnp.float32).astype(jnp.bfloat16)
+
+        @pl.loop(0, n_cols)
+        def _(c):
+            slot = lax.rem(c, 2)
+            cols = pl.ds(pl.multiple_of(c * width, width), width)
+            if before is None:
+                @pl.when(c >= 2)
+                def _():
+                    put(r, c - 2, slot).wait()
+            else:
+                @pl.when(c >= 2)
+                def _():
+                    put(r, c - 2, slot).wait()
+
+                @pl.when(c < 2)
+                def _():
+                    put(before, n_cols - 2 + c, slot).wait()
+            rows = jnp.dot(pick[...], u_buf[r, :, cols], preferred_element_type=jnp.float32).astype(jnp.bfloat16)
+            for e in range(local):
+                stage[slot, e] = rows[e * capacity:(e + 1) * capacity, :]
+            put(r, c, slot).start()
+
+    dispatch(0, None)
+    tokens.arrive(tokens.mate)
+    dispatch(4, 0)
+    tokens.forward()
+    dispatch(1, 4)
+    dispatch(2, 1)
+    tokens.arrive(tokens.near_mate)
+    dispatch(5, 2)
+    tokens.forward_far()
+    dispatch(6, 5)
+    dispatch(3, 6)
+    tokens.arrive(tokens.far_mate)
+    dispatch(7, 3)
+    gates.arrive(gates.own + gates.mate)
+    for copy in gates.near_mate:
+        copy.start()
+    gates.forward_far()
+    gates.arrive(gates.near_mate + gates.far_mate)
+    for r in range(group):
+        gates_ref[r] = g_buf[r]
+    for c in range(n_cols - 2, n_cols):
+        put(7, c, c % 2).wait()
+    tokens.finish()
+    gates.finish()
+
+
+def dispatch_tokens(h, router_t, ids_t, rank, capacity):
+    n_tok, d_model = h.shape
+    group, local = rank.shape[:2]
+    top_k = ids_t.shape[0]
     width = 512
-    for c in range(u_ref.shape[2] // width):
-        cols = slice(c * width, (c + 1) * width)
-        rows = jnp.dot(pick, u_ref[0, :, cols], preferred_element_type=jnp.float32).astype(jnp.bfloat16)
-        for e in range(local):
-            x_ref[0, e, :, cols] = rows[e * capacity:(e + 1) * capacity, :]
-
-
-def dispatch(order, rank, tokens, capacity):
-    n_src, local, n_tok = rank.shape
-    d_model = tokens.shape[2]
+    vmem = pl.BlockSpec(memory_space=pltpu.VMEM)
     return pl.pallas_call(
-        functools.partial(dispatch_kernel, capacity=capacity),
-        grid_spec=pltpu.PrefetchScalarGridSpec(
-            num_scalar_prefetch=1,
-            grid=(n_src,),
-            in_specs=[pl.BlockSpec((1, local, n_tok), lambda s, order: (s, 0, 0)), pl.BlockSpec((1, n_tok, d_model), lambda s, order: (order[s], 0, 0))],
-            out_specs=pl.BlockSpec((1, local, capacity, d_model), lambda s, order: (s, 0, 0, 0)),
-        ),
-        out_shape=jax.ShapeDtypeStruct((n_src, local, capacity, d_model), jnp.bfloat16),
-        compiler_params=params(),
-        cost_estimate=pl.CostEstimate(flops=2 * n_src * local * capacity * n_tok * d_model, bytes_accessed=4 * n_src * local * capacity * d_model, transcendentals=0),
-        name="dispatch",
-    )(order, rank, tokens)
+        dispatch_kernel,
+        in_specs=[vmem] * 4,
+        out_specs=[pl.BlockSpec(memory_space=pl.ANY), vmem],
+        out_shape=[jax.ShapeDtypeStruct((group, local, capacity, d_model), jnp.bfloat16), jax.ShapeDtypeStruct((group, top_k, n_tok), jnp.float32)],
+        scratch_shapes=[
+            pltpu.VMEM((group, n_tok, d_model), jnp.bfloat16),
+            pltpu.VMEM((local * capacity, n_tok), jnp.bfloat16),
+            pltpu.VMEM((2, local, capacity, width), jnp.bfloat16),
+            pltpu.VMEM((group, top_k, n_tok), jnp.float32),
+            pltpu.SemaphoreType.DMA((2,)),
+            pltpu.SemaphoreType.DMA((9,)),
+            pltpu.SemaphoreType.DMA((9,)),
+            pltpu.SemaphoreType.DMA((9,)),
+            pltpu.SemaphoreType.DMA((9,)),
+        ],
+        compiler_params=pltpu.CompilerParams(vmem_limit_bytes=MAX_VMEM, collective_id=1, has_side_effects=True),
+        cost_estimate=pl.CostEstimate(flops=2 * group * local * capacity * n_tok * d_model, bytes_accessed=2 * group * local * capacity * d_model, transcendentals=0),
+        name="dispatch_tokens",
+    )(h, router_t, ids_t, rank)
 
 
 def expert_kernel(size_ref, start_ref, total_ref, x_ref, gate_ref, up_ref, down_ref, f_ref, x_buf, f_buf, in_sems, out_sems, *, chunk):
@@ -173,24 +424,6 @@
     )(sizes, starts, totals, rows, gate_w, up_w, down_w)
 
 
-def neighbour(chips, swap=False):
-    me, group = lax.axis_index('ep'), lax.axis_size('ep')
-    side = lax.rem(me, 2)
-    chip = lax.rem(me // 2 + chips + group // 2, group // 2)
-    return {'ep': chip * 2 + (1 - side if swap else side)}
-
-
-def greet():
-    barrier = pltpu.get_barrier_semaphore()
-    for device in (neighbour(1), neighbour(-1), neighbour(0, True)):
-        pl.semaphore_signal(barrier, inc=1, device_id=device, device_id_type=pl.DeviceIdType.MESH)
-    pl.semaphore_wait(barrier, 3)
-
-
-def remote(src, dst, send_sem, recv_sem, device):
-    return pltpu.make_async_remote_copy(src_ref=src, dst_ref=dst, send_sem=send_sem, recv_sem=recv_sem, device_id=device, device_id_type=pl.DeviceIdType.MESH)
-
-
 def reduce_kernel(rank_ref, piece_ref, f_ref, out_ref, f_buf, spread, other_buf, swap_buf, send_buf, ring_buf, f_sems, swap_send, swap_recv, ring_send, ring_recv, out_sems, free_sem):
     n_src, n_tok, local = rank_ref.shape
     capacity = f_ref.shape[2]
@@ -242,7 +475,7 @@
 
     for side in range(2):
         fetch(0, side, 0).start()
-    greet()
+    greet(neighbour(1), neighbour(-1), neighbour(0, True))
 
     @pl.loop(0, n_units)
     def _(i):
@@ -367,59 +600,36 @@
 
 def local_layer(x_loc, q_shard, k_shard, v_shard, o_shard, w_router, gate_loc, up_loc, down_loc, sgate_shard, sup_shard, sdown_shard, ids_loc, group):
     n_seq, seq_len, d_model = x_loc.shape
-    head = q_shard.shape[2]
+    assert n_seq == 1 and group == 8 and q_shard.shape[2] == 128
     n_tok = n_seq * seq_len
     top_k = ids_loc.shape[-1]
     local = gate_loc.shape[0]
     n_experts = local * group
     capacity = CAP_FACTOR * n_tok * top_k // n_experts
-    me = lax.axis_index('ep')
-    chips = [me // 2 + step for step in (0, -1, 1, 2)]
-    order = jnp.stack([(c % (group // 2)) * 2 + side for side in (me % 2, 1 - me % 2) for c in chips]).astype(jnp.int32)
-
     def gathered(shard):
         return lax.all_gather(shard.reshape(shard.shape[0], -1), 'ep', axis=0, tiled=True)
 
     def project(rows, weight):
         return jnp.dot(rows, weight, preferred_element_type=jnp.float32).astype(jnp.bfloat16)
 
-    ids_all = lax.all_gather(ids_loc.reshape(n_tok, top_k).T, 'ep', axis=0)[order]
+    x_flat = x_loc.reshape(n_tok, d_model)
+    ids_t = ids_loc.reshape(n_tok, top_k).T
+    residual, rank, ids_all = attention_layer(x_flat, ids_t, *[w.reshape(w.shape[0], -1) for w in (k_shard, v_shard, q_shard, o_shard)], group, local)
+    rows, gates_all = dispatch_tokens(residual, w_router.T, ids_t, rank, capacity)
+
+    rank_t = rank.transpose(0, 2, 1)
+    sizes = (jnp.max(rank, axis=2) + 1 + ALIGN - 1) // ALIGN * ALIGN
+    ends = jnp.cumsum(sizes, axis=0)
+    starts, totals = ends - sizes, ends[-1]
+    rows, sgate_shard, sup_shard, sdown_shard = lax.optimization_barrier((rows, sgate_shard, sup_shard, sdown_shard))
+    results = experts(sizes, starts, totals, rows, gate_loc, up_loc, down_loc)
+
     mine = lax.axis_index('ep') * local + jnp.arange(local)
     chosen = ids_all[:, None, :, :] == mine[None, :, None, None]
-    member = jnp.any(chosen, axis=2)
-    before = (jnp.arange(n_tok)[:, None] < jnp.arange(n_tok)[None, :]).astype(jnp.bfloat16)
-    rank = jnp.einsum('set,tq->seq', member.astype(jnp.bfloat16), before, preferred_element_type=jnp.float32).astype(jnp.int32)
-    rank = jnp.where(member, rank, -1)
-    rank_t = rank.transpose(0, 2, 1)
-    sizes = (jnp.sum(member.astype(jnp.int32), axis=2) + ALIGN - 1) // ALIGN * ALIGN
-    ends = jnp.cumsum(sizes, axis=0)
-    starts, totals = ends - sizes, ends[-1]
-
-    x_flat = x_loc.reshape(n_tok, d_model)
-    normed = rms_norm(x_flat).astype(jnp.bfloat16)
-    keys_all = project(normed, gathered(k_shard))
-    vals_all = project(normed, gathered(v_shard))
-    queries = project(normed, gathered(q_shard))
-    attended = [attention(queries[i * seq_len:(i + 1) * seq_len], keys_all[i * seq_len:(i + 1) * seq_len], vals_all[i * seq_len:(i + 1) * seq_len], head) for i in range(n_seq)]
-    attended = attended[0] if n_seq == 1 else jnp.concatenate(attended, axis=0)
-    attn_out = project(attended, gathered(o_shard))
-    residual = (x_flat.astype(jnp.float32) + attn_out.astype(jnp.float32)).astype(jnp.bfloat16)
-
-    hidden = rms_norm(residual)
-    moe_in = hidden.astype(jnp.bfloat16)
-    tokens = lax.all_gather(moe_in, 'ep', axis=0)
-    logits = jnp.dot(hidden, w_router, precision=lax.Precision.HIGHEST, preferred_element_type=jnp.float32)
-    tok_ids = ids_loc.reshape(n_tok, top_k)
-    picked = tok_ids[:, :, None] == jnp.arange(n_experts)[None, None, :]
-    chosen_logits = jnp.sum(jnp.where(picked, logits[:, None, :], 0.0), axis=2)
-    gate_probs = jax.nn.softmax(chosen_logits, axis=-1)
-    gates_all = lax.all_gather(gate_probs.T, 'ep', axis=0)[order]
     weight = jnp.sum(jnp.where(chosen, gates_all[:, None, :, :], 0.0), axis=2)
     pieces = jnp.concatenate(bf16_pieces(weight), axis=1).transpose(0, 2, 1)
 
-    rows = dispatch(order, rank, tokens, capacity)
-    results = experts(sizes, starts, totals, rows, gate_loc, up_loc, down_loc)
-
+    moe_in = rms_norm(residual).astype(jnp.bfloat16)
     gate_act = jnp.dot(moe_in, gathered(sgate_shard), preferred_element_type=jnp.float32)
     up_act = jnp.dot(moe_in, gathered(sup_shard), preferred_element_type=jnp.float32)
     middle = (jax.nn.silu(gate_act) * up_act).astype(jnp.bfloat16)

time: 619 us -> 543 us (0.88)
  waiting for transfers between devices: 200 us -> 1.53 us
  Pallas kernels: 288 us -> 486 us
  matrix products: 61.8 us -> 17.8 us
  blocking collectives: 26.3 us -> 0 us
    pallas_call x2, Pallas kernels: 44.2 us -> 242 us  [the longest x1 154 us: attention_layer(): pl.pallas_call(attention_layer_kernel, in_specs=[vmem] + [anywhere] * 5,...]
    all_gather x7 -> x3, waiting for transfers between devices: 144 us -> 0.02 us  [gathered(): lax.all_gather(shard.reshape(shard.shape[0], -1), 'ep', axis=0, tiled=True)]
    all_gather x1 -> x0, waiting for transfers between devices: 53 us -> none  [local_layer(): tokens = lax.all_gather(moe_in, 'ep', axis=0)]
    dot_general x5 -> x1, matrix products: 49.3 us -> 11.2 us  [project(): jnp.dot(rows, weight, preferred_element_type=jnp.float32)]
    all_gather x2 -> x0, blocking collectives: 26.3 us -> none  [the longest x1 13.2 us: local_layer(): lax.all_gather(ids_loc.reshape(n_tok, top_k).T, 'ep', axis=0)[order]]
    dot_general x2 -> x0, matrix products: 6.6 us -> none  [the longest x1 4.44 us: local_layer(): jnp.dot(hidden, w_router, precision=lax.Precision.HIGHEST, preferred_elem...]
  transfers between devices with their start and end apart: 8 -> 3, of which waited for: 5 -> 0; matrix products, arithmetic and copies ran while one was open for 11% -> 3% of each run, Pallas kernels for 47% -> 46%
where the time goes in v3:
time: 543 us; the launch traced here: 533 us
  Pallas kernels  486 us (90%)
  matrix products  17.8 us (3%)
  between operations  13.7 us (3%)
  local copies, waits for them, and re-layouts  10.2 us (2%)
    pallas_call x1, Pallas kernels, reduce_results(): pl.pallas_call(reduce_kernel, in_specs=[vmem, vmem, pl.BlockSpec(memory_s...  159 us
    pallas_call x1, Pallas kernels, attention_layer(): pl.pallas_call(attention_layer_kernel, in_specs=[vmem] + [anywhere] * 5,...  154 us
    pallas_call x1, Pallas kernels, dispatch_tokens(): pl.pallas_call(dispatch_kernel, in_specs=[vmem] * 4, out_specs=[pl.BlockS...  88 us
    pallas_call x1, Pallas kernels, experts(): pl.pallas_call(functools.partial(expert_kernel, chunk=chunk), grid_spec=p...  85.6 us
    dot_general x1, matrix products, project(): jnp.dot(rows, weight, preferred_element_type=jnp.float32)  11.2 us
  transfers between devices with their start and end apart: 3, of which 0 were waited for; matrix products, arithmetic and copies ran while one was open for 3% of the time, Pallas kernels for 46%

profile of v3, /device:TPU:81, one launch (start us, length us, event | category | flops | bytes accessed | tf_op | source)
XLA Modules:
  0.0 532.6 jit_solution(483443317520349610)
XLA Ops:
  6.6 2.5 copy.25
  9.0 3.4 copy_bitcast_fusion
  12.4 153.7 %attention_layer.1 = (bf16[512,2048]{1,0:T(8,128)(2,1)}, s32[8,8,512]{2,1,0:T(8,128)}, s32[8,8,512]{2,1,0:T(8,128)}) custom-call(bf16[512,2048]{1,0:T(8,128)(2,1)} %bitcast.30, s32[8,512]{1,0:T(8,128)} %bitcast.32, bf16[256,2048]{1,0:T(8,128)(2,1)} %bitcast.27, bf16[256,2048]{1,0:T(8,128)(2,1)} %get-tuple-element.27.v_hbm, ...), custom_call_target="tpu_custom_call" | custom-call | flops 19327352832 | bytes 4194304 | tf_op jit(solution)/shard_map/attention_layer/pallas_call | solution.py:202
  166.1 88.0 %dispatch_tokens.1 = (bf16[8,8,128,2048]{3,2,1,0:T(8,128)(2,1)}, f32[8,8,512]{2,1,0:T(8,128)}) custom-call(bf16[512,2048]{1,0:T(8,128)(2,1)} %get-tuple-element.14.h_ref, f32[64,2048]{1,0:T(8,128)} %bitcast.31, s32[8,512]{1,0:T(8,128)} %bitcast.33, s32[8,8,512]{2,1,0:T(8,128)} %get-tuple-element.15.rank_ref), custom_call_target="tpu_custom_call" | custom-call | flops 17179869184 | bytes 33554432 | tf_op jit(solution)/shard_map/dispatch_tokens/pallas_call | solution.py:314
  254.1 0.1 all-gather.4.cloned.1.call-update
  254.2 0.1 all-gather.6.cloned.1.call-start
  254.2 0.7 all-gather.6.cloned.1.call-update
  255.0 0.1 all-gather.8.cloned.1.call-start
  255.0 0.7 all-gather.8.cloned.1.call-update
  255.8 1.1 reduce_max.9
  256.9 0.0 copy-start.5
  256.9 0.6 fusion.14.start_ref
  257.5 0.5 slice_bitcast_fusion.total_ref
  258.1 85.6 %experts.1.f_ref = bf16[8,8,128,2048]{3,2,1,0:T(8,128)(2,1)} custom-call(s32[8,8]{1,0:T(8,128)} %copy-done.5, s32[8,8]{1,0:T(8,128)} %fusion.14.start_ref, s32[8]{0:T(128)} %slice_bitcast_fusion.total_ref, bf16[8,8,128,2048]{3,2,1,0:T(8,128)(2,1)} %get-tuple-element.19.x_ref, bf16[8,2048,1024]{2,1,0:T(8,128)(2,1)} %gate_ref.1, ...), custom_call_target="tpu_custom_call" | custom-call | flops 68719476736 | bytes 100663296 | tf_op jit(solution)/shard_map/experts/pallas_call | solution.py:402
  343.7 0.0 copy-done.2
  343.7 1.9 copy.17
  345.6 0.4 select_reduce_fusion
  346.1 1.9 copy.18
  348.0 0.5 fusion.2
  348.5 0.6 add_rsqrt_fusion
  349.0 158.8 %reduce_results.1 = f32[512,2048]{1,0:T(8,128)} custom-call(s32[8,512,8]{2,1,0:T(8,128)} %bitcast.25, f32[8,512,24]{2,1,0:T(8,128)} %bitcast.24, bf16[8,8,128,2048]{3,2,1,0:T(8,128)(2,1)} %experts.1.f_ref), custom_call_target="tpu_custom_call" | custom-call | flops 51539607552 | bytes 67108864 | tf_op jit(solution)/shard_map/reduce_results/pallas_call | solution.py:568
  507.8 0.0 all-gather.4.cloned.1.call-done
  507.9 6.6 %fusion.6 = f32[512,1024]{1,0:T(8,128)} fusion(bf16[2048,1024]{1,0:T(8,128)(2,1)} %all-gather.4.cloned.1.call-done, bf16[512,2048]{1,0:T(8,128)(2,1)} %get-tuple-element.14.h_ref, f32[512]{0:T(512)} %add_rsqrt_fusion), kind=kOutput, calls=%fused_computation.14 | convolution fusion | flops 2150629376 | bytes 8390656 | tf_op jit(solution)/shard_map/dot_general | solution.py:633
  514.5 11.2 %fusion.4 = bf16[1,512,2048]{2,1,0:T(8,128)(2,1)} fusion(bf16[1024,2048]{1,0:T(8,128)(2,1)} %all-gather.8.cloned.1.call-done, f32[512,2048]{1,0:T(8,128)} %reduce_results.1, bf16[512,2048]{1,0:T(8,128)(2,1)S(1)} %copy-done.1, f32[512,1024]{1,0:T(8,128)} %fusion.6, bf16[2048,1024]{1,0:T(8,128)(2,1)} %all-gather.6.cloned.1.call-done, f32[512]{0:T(512)S(1)} %copy-done.6), kind=kOutput, calls=%fused_computation.8 | convolution fusion | flops 4307550208 | bytes 18876416 | tf_op jit(solution)/shard_map/dot_general | solution.py:613
  (20 shorter events, 0.1 us)
Async XLA Ops:
  6.5 501.3 %all-gather.4.cloned.1.call-start = ((), (), s32[]{:S(2)}) async-start(), calls=%async_computation | async-start | bytes 4718592 | tf_op jit(solution)/shard_map/all_gather | solution.py:610
  254.2 260.3 %all-gather.6.cloned.1.call-start = ((), (), s32[]{:S(2)}) async-start(), calls=%async_computation.1 | async-start | bytes 4718592 | tf_op jit(solution)/shard_map/all_gather | solution.py:610
  255.0 259.5 %all-gather.8.cloned.1.call-start = ((), (), s32[]{:S(2)}) async-start(), calls=%async_computation.2 | async-start | bytes 4718592 | tf_op jit(solution)/shard_map/all_gather | solution.py:610
  256.9 1.2 copy-start.5
  258.1 85.6 %copy-start.2 = (s32[8,8,512]{2,1,0:T(8,128)S(1)}, s32[8,8,512]{2,1,0:T(8,128)}, u32[]{:S(2)}) copy-start(s32[8,8,512]{2,1,0:T(8,128)} %get-tuple-element.15.rank_ref) | copy-start | bytes 393220
  258.1 87.5 %copy-start.3 = (s32[8,8,512]{2,1,0:T(8,128)S(1)}, s32[8,8,512]{2,1,0:T(8,128)}, u32[]{:S(2)}) copy-start(s32[8,8,512]{2,1,0:T(8,128)} %get-tuple-element.16) | copy-start | bytes 393220
  258.1 87.5 %copy-start.4 = (f32[8,8,512]{2,1,0:T(8,128)S(1)}, f32[8,8,512]{2,1,0:T(8,128)}, u32[]{:S(2)}) copy-start(f32[8,8,512]{2,1,0:T(8,128)} %get-tuple-element.17) | copy-start | bytes 393220
  343.6 4.3 copy-start
  507.8 6.7 %copy-start.1 = (bf16[512,2048]{1,0:T(8,128)(2,1)S(1)}, bf16[512,2048]{1,0:T(8,128)(2,1)}, u32[]{:S(2)}) copy-start(bf16[512,2048]{1,0:T(8,128)(2,1)} %get-tuple-element.14.h_ref) | copy-start | bytes 6291460
  507.8 6.7 %copy-start.6 = (f32[512]{0:T(512)S(1)}, f32[512]{0:T(512)}, u32[]{:S(2)}) copy-start(f32[512]{0:T(512)} %add_rsqrt_fusion) | copy-start | bytes 6148
Sparse Core Ops, SparseCore 0:
  254.3 31.8 all-gather.3
  287.8 28.6 all-gather.5
  318.1 28.6 all-gather.7
